TPU v7x, 512 devices: a whole 4x4x16 slice. The times are simulated.
512 devices in a mesh: section: 16 (over y, x), seq: 8 (over z_lo, core), dp: 4 (over z_hi).
Axes of the slice: x: 4, y: 4, z: 16 (z_hi: 4, z_lo: 4; z = z_hi * 4 + z_lo), core: 2. Of those that a mesh axis runs over, the one named last changes fastest.
Arguments:
- stream: bfloat16 [16, 4, 1024, 1280], P('section', 'dp', 'seq'), may hold values from -16 to 16
- norm_gain: float32 [16, 1280], P('section'), may hold values from 0.25 to 1.75
- w_xbc: bfloat16 [16, 1280, 2688], P('section', ('seq', 'dp')), may hold values from -0.15625 to 0.15625
- w_dt: bfloat16 [16, 1280, 40], P('section', ('seq', 'dp')), may hold values from -0.15625 to 0.15625
- conv_weight: float32 [16, 4, 2688], P('section'), may hold values from -3 to 3
- conv_bias: float32 [16, 2688], P('section'), may hold values from -1.8 to 1.8
- dt_bias: float32 [16, 40], P('section'), may hold values from -1 to 1
- decay_rate: float32 [16, 40], P('section'), may hold values from 9.765625e-05 to 0.04
- skip_weight: float32 [16, 40], P('section'), may hold values from 0.5 to 1.5
- inner_gain: float32 [16, 2560], P('section'), may hold values from 0.25 to 1.75
- w_out: bfloat16 [16, 2560, 1280], P('section', ('seq', 'dp')), may hold values from -0.125 to 0.125
Outputs:
- next_stream: bfloat16 [16, 4, 1024, 1280], P('section', 'dp', 'seq')
All inputs are finite; a program needn't handle non-finite values.
Results may differ from a plain program's by a relative error of at most 0.008.
Values may be sent and summed in bfloat16 or wider, within the bound.
No kernel may reach another device: no remote copies, remote signals or barrier semaphores. Data moves between devices by JAX's collectives and lax.ppermute only.
A program may use at most 64 MiB of HBM per device.

v0:
```python
import jax
import jax.numpy as jnp
from jax import lax
from jax.experimental import pallas as pl
from jax.experimental.pallas import tpu as pltpu
from jax.sharding import Mesh
from jax.sharding import PartitionSpec as P

HEADS = 40
HEAD_DIM = 64
STATE = 64
CONV = 4
BLOCK = 128
INNER = 2560
D = 1280
SEQ = ("blk", "par", "core")
SEQ_DP = ("blk", "par", "core", "dp")
RING = ("blk", "core", "dp")
epsilon = 1e-05
LOCAL_HEADS = 10
LOCAL = LOCAL_HEADS * HEAD_DIM
TAPPED = LOCAL + 2 * STATE
WIDE = TAPPED + 128
ROWS = 512
PIECE = ROWS // BLOCK


def ring_index(place, core):
    place = place % 8
    return (place % 2) * 8 + core * 4 + place // 2


def shifted(x, by):
    pairs = []
    for i in range(8):
        pairs.append((ring_index(i, 0), ring_index(i + by, 0)))
        pairs.append((ring_index(i, 1), ring_index(i - by, 1)))
    return lax.ppermute(x, RING, pairs)


def gathered(x, cut):
    up, down = x, x
    out = [x]
    for _ in range(1, 4):
        up, down = shifted(up, 1), shifted(down, -1)
        out += [up, down]
    half = x.shape[cut] // 2
    first = lax.slice_in_dim(up, 0, half, axis=cut)
    second = lax.slice_in_dim(down, half, 2 * half, axis=cut)
    out += [shifted(first, 1), shifted(second, -1)]
    return out


OFFSETS = (0, -1, 1, -2, 2, -3, 3, 4, 4)


def slot_of(place, offset):
    there = (place + offset + 8) % 8
    return (there % 2) * 4 + there // 2


def fill(where, chunks, scratch, cut):
    rows = chunks[0].shape[0]
    place, sign = where[0], where[1]
    for k in range(7):
        at = pl.multiple_of(slot_of(place, OFFSETS[k] * sign) * rows, 16)
        scratch[pl.ds(at, rows), :] = chunks[k][...]
    at = slot_of(place, 4) * rows
    if cut == 0:
        half = rows // 2
        scratch[pl.ds(pl.multiple_of(at, 16), half), :] = chunks[7][...]
        scratch[pl.ds(pl.multiple_of(at + half, 16), half), :] = chunks[8][...]
    else:
        half = chunks[7].shape[1]
        at = pl.multiple_of(at, 16)
        scratch[pl.ds(at, rows), :half] = chunks[7][...]
        scratch[pl.ds(at, rows), half:] = chunks[8][...]


def exact_dot(a, b):
    return jnp.dot(a, b, preferred_element_type=jnp.float32, precision=lax.Precision.HIGHEST)


def spread(per_head):
    rows = per_head.shape[0]
    left = lax.broadcasted_iota(jnp.int32, (rows, 128), 1) < HEAD_DIM
    pairs = []
    for p in range(LOCAL_HEADS // 2):
        first = jnp.broadcast_to(per_head[:, 2 * p : 2 * p + 1], (rows, 128))
        second = jnp.broadcast_to(per_head[:, 2 * p + 1 : 2 * p + 2], (rows, 128))
        pairs.append(jnp.where(left, first, second))
    return jnp.concatenate(pairs, axis=1)


def class_columns(x, group, width):
    found = None
    for g in range(4):
        piece = jnp.concatenate(
            [x[:, g * width : (g + 1) * width], x[:, (g + 4) * width : (g + 5) * width]], axis=1
        )
        found = piece if found is None else jnp.where(group == g, piece, found)
    return found


def class_heads(x, group, width, lanes):
    head = lax.broadcasted_iota(jnp.int32, (HEADS, lanes), 0)
    local = lax.broadcasted_iota(jnp.int32, (HEADS, lanes), 1) // width
    wanted = jnp.where(local < 5, group * 5 + local, 15 + group * 5 + local)
    select = jnp.logical_and(local < LOCAL_HEADS, head == wanted)
    return exact_dot(x, select.astype(jnp.float32))


def mix_kernel(where, rows, halo, all_taps, all_bias, all_dt_bias, all_rate, all_skip, *rest):
    chunks, (y_out, c_out, grown_out, state_out, weight, raw) = rest[:9], rest[9:]
    fill(where, chunks, weight, 0)
    group = where[2]
    taps = jnp.concatenate(
        [class_columns(all_taps[0], group, 320), all_taps[0, :, INNER:]], axis=1
    )
    bias = jnp.concatenate(
        [class_columns(all_bias[...], group, 320), all_bias[:, INNER:]], axis=1
    )
    dt_bias = class_heads(all_dt_bias[...], group, 1, 128)
    rate = class_heads(all_rate[...], group, 1, 128)
    skip = class_heads(all_skip[...], group, HEAD_DIM, LOCAL)
    projected = jnp.dot(rows[...], weight[...], preferred_element_type=jnp.float32)
    before = jnp.dot(halo[...], weight[:, :TAPPED], preferred_element_type=jnp.float32)
    raw[:8, :] = before.astype(jnp.bfloat16).astype(jnp.float32)
    raw[8:, :] = projected[:, :TAPPED].astype(jnp.bfloat16).astype(jnp.float32)
    shift = projected[:, TAPPED:] + dt_bias
    dt_all = jnp.maximum(shift, 0.0) + jnp.log1p(jnp.exp(-jnp.abs(shift)))
    row_id = lax.broadcasted_iota(jnp.int32, (BLOCK, BLOCK), 0)
    col_id = lax.broadcasted_iota(jnp.int32, (BLOCK, BLOCK), 1)
    causal = row_id >= col_id
    lower = causal.astype(jnp.float32)
    left = col_id < HEAD_DIM
    state = jnp.zeros((STATE, LOCAL), jnp.float32)
    decayed = jnp.ones((1, LOCAL), jnp.float32)
    for n in range(PIECE):
        at = n * BLOCK
        conv = bias + taps[0:1, :] * raw[at + 5 : at + 5 + BLOCK, :]
        for k in range(1, CONV):
            conv = conv + taps[k : k + 1, :] * raw[at + 5 + k : at + 5 + k + BLOCK, :]
        xbc = (conv / (1.0 + jnp.exp(-conv))).astype(jnp.bfloat16)
        values = xbc[:, :LOCAL]
        both = xbc[:, LOCAL:]
        b_rows, c_rows = both[:, :STATE], both[:, STATE:]
        dt = dt_all[at : at + BLOCK, :]
        cum = exact_dot(lower, -dt * rate)
        cum_t, dt_t = cum.T, dt.T
        scores = lax.dot_general(
            c_rows, b_rows, (((1,), (1,)), ((), ())), preferred_element_type=jnp.float32
        )
        scores = jnp.where(causal, scores, 0.0)
        intra = []
        for p in range(LOCAL_HEADS // 2):
            mixes = []
            for h in (2 * p, 2 * p + 1):
                lag = cum[:, h : h + 1] - cum_t[h : h + 1, :]
                weights = jnp.exp(jnp.minimum(lag, 0.0))
                mixes.append((scores * weights * dt_t[h : h + 1, :]).astype(jnp.bfloat16))
            pair = values[:, 128 * p : 128 * p + 128]
            none = jnp.zeros_like(pair)
            stacked = jnp.concatenate(
                [jnp.where(left, pair, none), jnp.where(left, none, pair)], axis=0
            )
            intra.append(
                jnp.dot(
                    jnp.concatenate(mixes, axis=1), stacked, preferred_element_type=jnp.float32
                )
            )
        wide = values.astype(jnp.float32)
        tail = spread(jnp.exp(cum[BLOCK - 1 :, :] - cum) * dt)
        growth = spread(jnp.exp(cum))
        scaled = (wide * tail).astype(jnp.bfloat16)
        local = jnp.concatenate(intra, axis=1) + skip * wide
        if n > 0:
            local = local + growth * exact_dot(c_rows.astype(jnp.float32), state)
        y_out[at : at + BLOCK, :] = local
        c_out[at : at + BLOCK, :] = c_rows
        grown_out[at : at + BLOCK, :] = growth * decayed
        summary = lax.dot_general(
            b_rows, scaled, (((0,), (0,)), ((), ())), preferred_element_type=jnp.float32
        )
        total = growth[BLOCK - 1 :, :]
        state = total * state + summary
        decayed = decayed * total
    state_out[...] = state.astype(jnp.bfloat16)


def late_kernel(y_in, c_in, grown, arriving, y_out, square_out):
    y = y_in[...] + grown[...] * jnp.dot(
        c_in[...], arriving[...], preferred_element_type=jnp.float32
    )
    y_out[...] = y
    square_out[...] = jnp.broadcast_to(jnp.sum(y * y, axis=1, keepdims=True), (ROWS, 128))


def out_kernel(where, y_in, square, all_gain, *rest):
    chunks, (out, weight) = rest[:9], rest[9:]
    fill(where, chunks, weight, 1)
    gain = class_columns(all_gain[...], where[2], 320)
    scale = lax.rsqrt(square[:, :1] * (1.0 / INNER) + epsilon)
    normed = (y_in[...] * scale * gain).astype(jnp.bfloat16)
    out[...] = jnp.dot(normed, weight[...], preferred_element_type=jnp.float32).astype(jnp.bfloat16)


VMEM = pl.BlockSpec(memory_space=pltpu.VMEM)
SMEM = pl.BlockSpec(memory_space=pltpu.SMEM)


def call(kernel, outs, scratch, scalars, *arrays):
    return pl.pallas_call(
        kernel,
        out_shape=outs,
        in_specs=[SMEM] * len(scalars) + [VMEM] * len(arrays),
        out_specs=jax.tree.map(lambda _: VMEM, outs),
        scratch_shapes=scratch,
        compiler_params=pltpu.CompilerParams(vmem_limit_bytes=40 * 1024 * 1024),
    )(*scalars, *arrays)


def swapped(x, axis):
    return lax.ppermute(x, axis, [(0, 1), (1, 0)])


def both_of(mine, theirs, index):
    first = jnp.where(index == 0, mine, theirs)
    second = jnp.where(index == 0, theirs, mine)
    return jnp.stack([first, second])


def shards(
    stream,
    norm_gain,
    w_xbc,
    w_dt,
    conv_weight,
    conv_bias,
    dt_bias,
    decay_rate,
    skip_weight,
    inner_gain,
    w_out,
):
    par, core = lax.axis_index("par"), lax.axis_index("core")
    group = par * 2 + core
    place = lax.axis_index("dp") * 2 + lax.axis_index("blk")
    where = jnp.stack([place, 1 - 2 * core, group]).astype(jnp.int32)

    out_chunks = gathered(w_out[0], 1)
    xbc, dtw = w_xbc[0], w_dt[0]
    inner = xbc[:, :INNER].reshape(40, 2, 4, 320).transpose(2, 0, 1, 3).reshape(4, 40, LOCAL)
    shared = jnp.broadcast_to(xbc[None, :, INNER:], (4, 40, 2 * STATE))
    steps = dtw.reshape(40, 2, 4, 5).transpose(2, 0, 1, 3).reshape(4, 40, LOCAL_HEADS)
    steps = jnp.pad(steps, ((0, 0), (0, 0), (0, 128 - LOCAL_HEADS)))
    packed = jnp.concatenate([inner, shared, steps], axis=2)
    classes = lax.all_to_all(packed, ("par", "core"), 0, 0).reshape(160, WIDE)
    in_chunks = gathered(classes, 0)

    rows_in = stream[0, 0]
    wide = rows_in.astype(jnp.float32)
    mean_square = jnp.mean(wide * wide, axis=-1, keepdims=True)
    normed = (wide * lax.rsqrt(mean_square + epsilon) * norm_gain[0]).astype(jnp.bfloat16)
    feature = lax.broadcasted_iota(jnp.int32, (D, D), 0)
    target = lax.broadcasted_iota(jnp.int32, (D, D), 1)
    source = (target // 640) * 640 + (target // 40 % 4) * 160 + (target // 160 % 4) * 40 + target % 40
    select = (feature == source).astype(jnp.bfloat16)
    normed = jnp.dot(normed, select, preferred_element_type=jnp.float32).astype(jnp.bfloat16)
    pair = both_of(normed, swapped(normed, "par"), par)
    quad = both_of(pair, swapped(pair, "core"), core)
    rows = quad.transpose(1, 0, 2, 3).reshape(ROWS, D)
    halo = lax.ppermute(rows[ROWS - 8 :], "blk", [(0, 1)])

    f32, bf16 = jnp.float32, jnp.bfloat16
    y_local, c_rows, grown, state = call(
        mix_kernel,
        (
            jax.ShapeDtypeStruct((ROWS, LOCAL), f32),
            jax.ShapeDtypeStruct((ROWS, STATE), bf16),
            jax.ShapeDtypeStruct((ROWS, LOCAL), f32),
            jax.ShapeDtypeStruct((STATE, LOCAL), bf16),
        ),
        [pltpu.VMEM((D, WIDE), bf16), pltpu.VMEM((ROWS + 8, TAPPED), f32)],
        (where,),
        rows,
        halo,
        conv_weight,
        conv_bias,
        dt_bias,
        decay_rate,
        skip_weight,
        *in_chunks,
    )
    arriving = lax.ppermute(state, "blk", [(0, 1)])
    y, square = call(
        late_kernel,
        (jax.ShapeDtypeStruct((ROWS, LOCAL), f32), jax.ShapeDtypeStruct((ROWS, 128), f32)),
        [],
        (),
        y_local,
        c_rows,
        grown,
        arriving,
    )
    square = square[:, 0].reshape(PIECE, BLOCK)
    square = square + swapped(square, "core")
    square = square + swapped(square, "par")
    square = jnp.broadcast_to(square.reshape(ROWS, 1), (ROWS, 128))
    partial = call(
        out_kernel,
        jax.ShapeDtypeStruct((ROWS, D), bf16),
        [pltpu.VMEM((LOCAL, D), bf16)],
        (where,),
        y,
        square,
        inner_gain,
        *out_chunks,
    ).reshape(2, 2, BLOCK, D)

    own = jnp.where(core == 0, partial[:, 0], partial[:, 1])
    other = jnp.where(core == 0, partial[:, 1], partial[:, 0])
    chip = own.astype(f32) + swapped(other, "core").astype(f32)
    own = jnp.where(par == 0, chip[0], chip[1])
    other = jnp.where(par == 0, chip[1], chip[0]).astype(bf16)
    branch = own + swapped(other, "par").astype(f32)
    next_rows = (wide + branch).astype(bf16)
    moved = lax.ppermute(next_rows, "section", [(i, (i + 1) % 16) for i in range(16)])
    return moved[None, None]


def solution(mesh):
    torus = Mesh(
        mesh.devices.reshape(mesh.shape["section"], 2, 2, 2, mesh.shape["dp"]),
        ("section", "blk", "par", "core", "dp"),
    )
    return jax.shard_map(
        shards,
        mesh=torus,
        in_specs=(
            P("section", "dp", SEQ, None),
            P("section", None),
            P("section", SEQ_DP, None),
            P("section", SEQ_DP, None),
            P("section", None, None),
            P("section", None),
            P("section", None),
            P("section", None),
            P("section", None),
            P("section", None),
            P("section", SEQ_DP, None),
        ),
        out_specs=P("section", "dp", SEQ, None),
        check_vma=False,
    )
```

profile of v0, /device:TPU:1, one launch (start us, length us, event | category | flops | bytes accessed | tf_op | source)
XLA Modules:
  0.0 181.4 jit_solution(1541836067184711397)
XLA Ops:
  1.9 2.6 %fusion.28 = bf16[128,1280]{1,0:T(8,128)(2,1)S(1)} fusion(s32[1280]{0:T(1024)S(1)} %get-tuple-element.23, s32[1280]{0:T(1024)S(1)} %get-tuple-element.25, s32[1280]{0:T(1024)S(1)} %get-tuple-element.21, s32[1280]{0:T(1024)S(1)} %get-tuple-element.26, s32[1280]{0:T(1024)S(1)} %get-tuple-element.22, s32[1280]{0:T(1024)S(1)} %get-tuple-element.31, ...), kind=kOutput, calls=%fused_computation.37 | convolution fusion | flops 474316800 | bytes 707072 | tf_op jit(solution)/shard_map/dot_general | solution.py:269
  4.6 4.4 %collective-permute-start = (bf16[128,1280]{1,0:T(8,128)(2,1)S(1)}, bf16[128,1280]{1,0:T(8,128)(2,1)S(1)}, u32[]{:S(2)}, u32[]{:S(2)}) collective-permute-start(bf16[128,1280]{1,0:T(8,128)(2,1)S(1)} %fusion.28), channel_id=1, source_target_pairs={{0,8},{8,0},{1,9},{9,1},{2,10},{10,2},{3,11},{11,3},{4,12},{12,4},... | collective-permute-start | bytes 983048 | tf_op jit(solution)/shard_map/ppermute | solution.py:224
  10.6 7.8 %all-to-all-start = ((bf16[4,40,896]{2,1,0:T(8,128)(2,1)}), bf16[4,40,896]{2,1,0:T(8,128)(2,1)S(1)}, u32[]{:S(2)}, u32[]{:S(2)}) async-start(bf16[4,40,896]{2,1,0:T(8,128)(2,1)} %fusion.41), calls=%async_computation | async-start | bytes 573440 | tf_op jit(solution)/shard_map/all_to_all | solution.py:258
  18.6 3.8 %collective-permute-start.1 = (bf16[2,128,1280]{2,1,0:T(8,128)(2,1)S(1)}, bf16[2,128,1280]{2,1,0:T(8,128)(2,1)}, u32[]{:S(2)}, u32[]{:S(2)}) collective-permute-start(bf16[2,128,1280]{2,1,0:T(8,128)(2,1)S(1)} %pad_maximum_fusion), channel_id=1, source_target_pairs={{0,4},{4,0},{1,5},{5,1},{2,6},{6,2},{3,7},{7,3},{8,12},{12,8},{9,1... | collective-permute-start | bytes 1966088 | tf_op jit(solution)/shard_map/ppermute | solution.py:224
  25.7 7.4 %collective-permute-start.3 = (bf16[160,896]{1,0:T(8,128)(2,1)S(1)}, bf16[160,896]{1,0:T(8,128)(2,1)S(1)}, u32[]{:S(2)}, u32[]{:S(2)}) collective-permute-start(bf16[160,896]{1,0:T(8,128)(2,1)S(1)} %bitcast.66), channel_id=1, source_target_pairs={{0,16},{4,23},{16,1},{20,4},{1,17},{5,20},{17,2},{21,5},{2,18},{6,... | collective-permute-start | bytes 860168 | tf_op jit(solution)/shard_map/ppermute | solution.py:38
  33.1 2.2 %collective-permute-done.4.rest_2_ = bf16[160,896]{1,0:T(8,128)(2,1)S(1)} collective-permute-done((bf16[160,896]{1,0:T(8,128)(2,1)S(1)}, bf16[160,896]{1,0:T(8,128)(2,1)S(1)}, u32[]{:S(2)}, u32[]{:S(2)}) %collective-permute-start.4) | collective-permute-done | bytes 286752 | tf_op jit(solution)/shard_map/ppermute | solution.py:38
  35.3 6.8 %collective-permute-start.6 = (bf16[160,896]{1,0:T(8,128)(2,1)S(1)}, bf16[160,896]{1,0:T(8,128)(2,1)S(1)}, u32[]{:S(2)}, u32[]{:S(2)}) collective-permute-start(bf16[160,896]{1,0:T(8,128)(2,1)S(1)} %collective-permute-done.4.rest_2_), channel_id=1, source_target_pairs={{0,19},{4,20},{16,0},{20,5},{1,16},{5,21},{17,1},{21,6},{2,17},{6,... | collective-permute-start | bytes 860168 | tf_op jit(solution)/shard_map/ppermute | solution.py:38
  42.9 8.2 %collective-permute-start.5 = (bf16[160,896]{1,0:T(8,128)(2,1)S(1)}, bf16[160,896]{1,0:T(8,128)(2,1)S(1)}, u32[]{:S(2)}, u32[]{:S(2)}) collective-permute-start(bf16[160,896]{1,0:T(8,128)(2,1)S(1)} %collective-permute-done.3.rest_1_), channel_id=1, source_target_pairs={{0,16},{4,23},{16,1},{20,4},{1,17},{5,20},{17,2},{21,5},{2,18},{6,... | collective-permute-start | bytes 860168 | tf_op jit(solution)/shard_map/ppermute | solution.py:38
  53.1 4.3 %collective-permute-start.15 = (bf16[80,1280]{1,0:T(8,128)(2,1)S(1)}, bf16[80,1280]{1,0:T(8,128)(2,1)S(1)}, u32[]{:S(2)}, u32[]{:S(2)}) collective-permute-start(bf16[80,1280]{1,0:T(8,128)(2,1)S(1)} %bitcast.69), channel_id=1, source_target_pairs={{0,19},{4,20},{16,0},{20,5},{1,16},{5,21},{17,1},{21,6},{2,17},{6,... | collective-permute-start | bytes 614408 | tf_op jit(solution)/shard_map/ppermute | solution.py:38
  57.4 1.9 %collective-permute-start.8 = (bf16[160,896]{1,0:T(8,128)(2,1)S(1)}, bf16[160,896]{1,0:T(8,128)(2,1)S(1)}, u32[]{:S(2)}, u32[]{:S(2)}) collective-permute-start(bf16[160,896]{1,0:T(8,128)(2,1)S(1)} %collective-permute-done.6.rest_4_), channel_id=1, source_target_pairs={{0,19},{4,20},{16,0},{20,5},{1,16},{5,21},{17,1},{21,6},{2,17},{6,... | collective-permute-start | bytes 860168 | tf_op jit(solution)/shard_map/ppermute | solution.py:38
  60.6 6.3 %collective-permute-start.7 = (bf16[160,896]{1,0:T(8,128)(2,1)S(1)}, bf16[160,896]{1,0:T(8,128)(2,1)S(1)}, u32[]{:S(2)}, u32[]{:S(2)}) collective-permute-start(bf16[160,896]{1,0:T(8,128)(2,1)S(1)} %collective-permute-done.5.rest_3_), channel_id=1, source_target_pairs={{0,16},{4,23},{16,1},{20,4},{1,17},{5,20},{17,2},{21,5},{2,18},{6,... | collective-permute-start | bytes 860168 | tf_op jit(solution)/shard_map/ppermute | solution.py:38
  68.2 3.5 %collective-permute-done.8.rest_6_ = bf16[160,896]{1,0:T(8,128)(2,1)S(1)} collective-permute-done((bf16[160,896]{1,0:T(8,128)(2,1)S(1)}, bf16[160,896]{1,0:T(8,128)(2,1)S(1)}, u32[]{:S(2)}, u32[]{:S(2)}) %collective-permute-start.8) | collective-permute-done | bytes 286752 | tf_op jit(solution)/shard_map/ppermute | solution.py:38
  71.7 1.9 %collective-permute-start.10 = (bf16[80,896]{1,0:T(8,128)(2,1)S(1)}, bf16[80,896]{1,0:T(8,128)(2,1)S(1)}, u32[]{:S(2)}, u32[]{:S(2)}) collective-permute-start(bf16[80,896]{1,0:T(8,128)(2,1)S(1)} %slice.56), channel_id=1, source_target_pairs={{0,19},{4,20},{16,0},{20,5},{1,16},{5,21},{17,1},{21,6},{2,17},{6,... | collective-permute-start | bytes 430088 | tf_op jit(solution)/shard_map/ppermute | solution.py:38
  73.6 9.1 %collective-permute-done.7.rest_5_ = bf16[160,896]{1,0:T(8,128)(2,1)S(1)} collective-permute-done((bf16[160,896]{1,0:T(8,128)(2,1)S(1)}, bf16[160,896]{1,0:T(8,128)(2,1)S(1)}, u32[]{:S(2)}, u32[]{:S(2)}) %collective-permute-start.7) | collective-permute-done | bytes 286752 | tf_op jit(solution)/shard_map/ppermute | solution.py:38
  82.7 6.0 %collective-permute-start.9 = (bf16[80,896]{1,0:T(8,128)(2,1)S(1)}, bf16[80,896]{1,0:T(8,128)(2,1)S(1)}, u32[]{:S(2)}, u32[]{:S(2)}) collective-permute-start(bf16[80,896]{1,0:T(8,128)(2,1)S(1)} %slice.55), channel_id=1, source_target_pairs={{0,16},{4,23},{16,1},{20,4},{1,17},{5,20},{17,2},{21,5},{2,18},{6,... | collective-permute-start | bytes 430088 | tf_op jit(solution)/shard_map/ppermute | solution.py:38
  91.3 3.3 %collective-permute-done.9.rest_7_ = bf16[80,896]{1,0:T(8,128)(2,1)S(1)} collective-permute-done((bf16[80,896]{1,0:T(8,128)(2,1)S(1)}, bf16[80,896]{1,0:T(8,128)(2,1)S(1)}, u32[]{:S(2)}, u32[]{:S(2)}) %collective-permute-start.9) | collective-permute-done | bytes 143392 | tf_op jit(solution)/shard_map/ppermute | solution.py:38
  94.6 7.9 %shard_map.109 = (f32[512,640]{1,0:T(8,128)S(1)}, bf16[512,64]{1,0:T(8,128)(2,1)S(1)}, f32[512,640]{1,0:T(8,128)S(1)}, bf16[64,640]{1,0:T(8,128)(2,1)S(1)}) custom-call(s32[3]{0:T(128)S(1)} %pad_add_fusion.where, bf16[512,1280]{1,0:T(8,128)(2,1)S(1)} %bitcast.64, bf16[8,1280]{1,0:T(8,128)(2,1)S(1)} %collective-permute-done.2.halo, ...), custom_call_target="tpu_custom_call" | custom-call | tf_op jit(solution)/shard_map/pallas_call | solution.py:213
  104.0 6.2 %collective-permute-start.16 = (bf16[80,1280]{1,0:T(8,128)(2,1)S(1)}, bf16[80,1280]{1,0:T(8,128)(2,1)S(1)}, u32[]{:S(2)}, u32[]{:S(2)}) collective-permute-start(bf16[80,1280]{1,0:T(8,128)(2,1)S(1)} %collective-permute-done.14.rest_1_), channel_id=1, source_target_pairs={{0,16},{4,23},{16,1},{20,4},{1,17},{5,20},{17,2},{21,5},{2,18},{6,... | collective-permute-start | bytes 614408 | tf_op jit(solution)/shard_map/ppermute | solution.py:38
  110.2 1.9 %collective-permute-start.17 = (bf16[80,1280]{1,0:T(8,128)(2,1)S(1)}, bf16[80,1280]{1,0:T(8,128)(2,1)S(1)}, u32[]{:S(2)}, u32[]{:S(2)}) collective-permute-start(bf16[80,1280]{1,0:T(8,128)(2,1)S(1)} %collective-permute-done.15.rest_2_), channel_id=1, source_target_pairs={{0,19},{4,20},{16,0},{20,5},{1,16},{5,21},{17,1},{21,6},{2,17},{6,... | collective-permute-start | bytes 614408 | tf_op jit(solution)/shard_map/ppermute | solution.py:38
  112.7 6.8 %collective-permute-start.12 = (f32[4,128]{1,0:T(4,128)S(1)}, f32[4,128]{1,0:T(4,128)S(1)}, u32[]{:S(2)}, u32[]{:S(2)}) collective-permute-start(f32[4,128]{1,0:T(4,128)S(1)} %bitcast.77), channel_id=1, source_target_pairs={{0,4},{4,0},{1,5},{5,1},{2,6},{6,2},{3,7},{7,3},{8,12},{12,8},{9,1... | collective-permute-start | bytes 6152 | tf_op jit(solution)/shard_map/ppermute | solution.py:224
  119.5 3.6 %collective-permute-start.18 = (bf16[80,1280]{1,0:T(8,128)(2,1)S(1)}, bf16[80,1280]{1,0:T(8,128)(2,1)S(1)}, u32[]{:S(2)}, u32[]{:S(2)}) collective-permute-start(bf16[80,1280]{1,0:T(8,128)(2,1)S(1)} %collective-permute-done.16.rest_3_), channel_id=1, source_target_pairs={{0,16},{4,23},{16,1},{20,4},{1,17},{5,20},{17,2},{21,5},{2,18},{6,... | collective-permute-start | bytes 614408 | tf_op jit(solution)/shard_map/ppermute | solution.py:38
  123.2 2.5 %collective-permute-start.19 = (bf16[80,1280]{1,0:T(8,128)(2,1)S(1)}, bf16[80,1280]{1,0:T(8,128)(2,1)S(1)}, u32[]{:S(2)}, u32[]{:S(2)}) collective-permute-start(bf16[80,1280]{1,0:T(8,128)(2,1)S(1)} %collective-permute-done.17.rest_4_), channel_id=1, source_target_pairs={{0,19},{4,20},{16,0},{20,5},{1,16},{5,21},{17,1},{21,6},{2,17},{6,... | collective-permute-start | bytes 614408 | tf_op jit(solution)/shard_map/ppermute | solution.py:38
  125.7 3.3 %collective-permute-start.13 = (f32[4,128]{1,0:T(4,128)S(1)}, f32[4,128]{1,0:T(4,128)S(1)}, u32[]{:S(2)}, u32[]{:S(2)}) collective-permute-start(f32[4,128]{1,0:T(4,128)S(1)} %bitcast_add_fusion.1), channel_id=1, source_target_pairs={{0,8},{8,0},{1,9},{9,1},{2,10},{10,2},{3,11},{11,3},{4,12},{12,4},... | collective-permute-start | bytes 6152 | tf_op jit(solution)/shard_map/ppermute | solution.py:224
  129.1 3.7 %collective-permute-start.20 = (bf16[80,640]{1,0:T(8,128)(2,1)S(1)}, bf16[80,640]{1,0:T(8,128)(2,1)S(1)}, u32[]{:S(2)}, u32[]{:S(2)}) collective-permute-start(bf16[80,640]{1,0:T(8,128)(2,1)S(1)} %slice.57), channel_id=1, source_target_pairs={{0,16},{4,23},{16,1},{20,4},{1,17},{5,20},{17,2},{21,5},{2,18},{6,... | collective-permute-start | bytes 307208 | tf_op jit(solution)/shard_map/ppermute | solution.py:38
  133.6 5.5 %collective-permute-start.21 = (bf16[80,640]{1,0:T(8,128)(2,1)S(1)}, bf16[80,640]{1,0:T(8,128)(2,1)S(1)}, u32[]{:S(2)}, u32[]{:S(2)}) collective-permute-start(bf16[80,640]{1,0:T(8,128)(2,1)S(1)} %slice.58), channel_id=1, source_target_pairs={{0,19},{4,20},{16,0},{20,5},{1,16},{5,21},{17,1},{21,6},{2,17},{6,... | collective-permute-start | bytes 307208 | tf_op jit(solution)/shard_map/ppermute | solution.py:38
  139.2 4.2 %collective-permute-done.21.rest_8_ = bf16[80,640]{1,0:T(8,128)(2,1)S(1)} collective-permute-done((bf16[80,640]{1,0:T(8,128)(2,1)S(1)}, bf16[80,640]{1,0:T(8,128)(2,1)S(1)}, u32[]{:S(2)}, u32[]{:S(2)}) %collective-permute-start.21) | collective-permute-done | bytes 102432 | tf_op jit(solution)/shard_map/ppermute | solution.py:38
  143.5 1.9 %shard_map.111 = bf16[512,1280]{1,0:T(8,128)(2,1)S(1)} custom-call(s32[3]{0:T(128)S(1)} %pad_add_fusion.where, f32[512,640]{1,0:T(8,128)S(1)} %get-tuple-element.15.y_in, f32[512,128]{1,0:T(8,128)S(1)} %broadcast_in_dim.19.square, f32[1,2560]{1,0:T(1,128)S(1)} %copy-done.3, bf16[80,1280]{1,0:T(8,128)(2,1)S(1)} %bitcast.70, ...), custom_call_target="tpu_custom_call" | custom-call | tf_op jit(solution)/shard_map/pallas_call | solution.py:213
  145.5 8.1 %collective-permute-start.22 = (bf16[2,128,1280]{2,1,0:T(8,128)(2,1)S(1)}, bf16[2,128,1280]{2,1,0:T(8,128)(2,1)S(1)}, u32[]{:S(2)}, u32[]{:S(2)}) collective-permute-start(bf16[2,128,1280]{2,1,0:T(8,128)(2,1)S(1)} %select_bitcast_fusion), channel_id=1, source_target_pairs={{0,4},{4,0},{1,5},{5,1},{2,6},{6,2},{3,7},{7,3},{8,12},{12,8},{9,1... | collective-permute-start | bytes 1966088 | tf_op jit(solution)/shard_map/ppermute | solution.py:224
  155.7 2.2 %collective-permute-start.23 = (bf16[128,1280]{1,0:T(8,128)(2,1)S(1)}, bf16[128,1280]{1,0:T(8,128)(2,1)S(1)}, u32[]{:S(2)}, u32[]{:S(2)}) collective-permute-start(bf16[128,1280]{1,0:T(8,128)(2,1)S(1)} %fusion.36), channel_id=1, source_target_pairs={{0,8},{8,0},{1,9},{9,1},{2,10},{10,2},{3,11},{11,3},{4,12},{12,4},... | collective-permute-start | bytes 983048 | tf_op jit(solution)/shard_map/ppermute | solution.py:224
  157.9 8.6 %collective-permute-done.23 = bf16[128,1280]{1,0:T(8,128)(2,1)S(1)} collective-permute-done((bf16[128,1280]{1,0:T(8,128)(2,1)S(1)}, bf16[128,1280]{1,0:T(8,128)(2,1)S(1)}, u32[]{:S(2)}, u32[]{:S(2)}) %collective-permute-start.23) | collective-permute-done | bytes 327712 | tf_op jit(solution)/shard_map/ppermute | solution.py:224
  166.6 3.4 %collective-permute-start.24 = (bf16[128,1280]{1,0:T(8,128)(2,1)S(1)}, bf16[128,1280]{1,0:T(8,128)(2,1)S(1)}, u32[]{:S(2)}, u32[]{:S(2)}) collective-permute-start(bf16[128,1280]{1,0:T(8,128)(2,1)S(1)} %fusion.34), channel_id=1, source_target_pairs={{0,32},{32,64},{64,96},{96,128},{128,160},{160,192},{192,224},{224... | collective-permute-start | bytes 983048 | tf_op jit(solution)/shard_map/ppermute | solution.py:328
  170.1 10.6 %collective-permute-done.24 = bf16[128,1280]{1,0:T(8,128)(2,1)S(1)} collective-permute-done((bf16[128,1280]{1,0:T(8,128)(2,1)S(1)}, bf16[128,1280]{1,0:T(8,128)(2,1)S(1)}, u32[]{:S(2)}, u32[]{:S(2)}) %collective-permute-start.24) | collective-permute-done | bytes 327712 | tf_op jit(solution)/shard_map/ppermute | solution.py:328
  (84 shorter events, 20.5 us)
Async XLA Ops:
  1.9 7.0 %copy-start.8 = (bf16[1,40,2688]{2,1,0:T(8,128)(2,1)S(1)}, bf16[1,40,2688]{2,1,0:T(8,128)(2,1)}, u32[]{:S(2)}) copy-start(bf16[1,40,2688]{2,1,0:T(8,128)(2,1)} %param.13) | copy-start | bytes 645124
  4.6 13.9 %collective-permute-start = (bf16[128,1280]{1,0:T(8,128)(2,1)S(1)}, bf16[128,1280]{1,0:T(8,128)(2,1)S(1)}, u32[]{:S(2)}, u32[]{:S(2)}) collective-permute-start(bf16[128,1280]{1,0:T(8,128)(2,1)S(1)} %fusion.28), channel_id=1, source_target_pairs={{0,8},{8,0},{1,9},{9,1},{2,10},{10,2},{3,11},{11,3},{4,12},{12,4},... | collective-permute-start | bytes 983048 | tf_op jit(solution)/shard_map/ppermute | solution.py:224
  10.6 13.1 %all-to-all-start = ((bf16[4,40,896]{2,1,0:T(8,128)(2,1)}), bf16[4,40,896]{2,1,0:T(8,128)(2,1)S(1)}, u32[]{:S(2)}, u32[]{:S(2)}) async-start(bf16[4,40,896]{2,1,0:T(8,128)(2,1)} %fusion.41), calls=%async_computation | async-start | bytes 573440 | tf_op jit(solution)/shard_map/all_to_all | solution.py:258
  18.5 32.7 %copy-start = (bf16[1,80,1280]{2,1,0:T(8,128)(2,1)S(1)}, bf16[1,80,1280]{2,1,0:T(8,128)(2,1)}, u32[]{:S(2)}) copy-start(bf16[1,80,1280]{2,1,0:T(8,128)(2,1)} %param.21) | copy-start | bytes 614404
  18.6 48.4 %collective-permute-start.1 = (bf16[2,128,1280]{2,1,0:T(8,128)(2,1)S(1)}, bf16[2,128,1280]{2,1,0:T(8,128)(2,1)}, u32[]{:S(2)}, u32[]{:S(2)}) collective-permute-start(bf16[2,128,1280]{2,1,0:T(8,128)(2,1)S(1)} %pad_maximum_fusion), channel_id=1, source_target_pairs={{0,4},{4,0},{1,5},{5,1},{2,6},{6,2},{3,7},{7,3},{8,12},{12,8},{9,1... | collective-permute-start | bytes 1966088 | tf_op jit(solution)/shard_map/ppermute | solution.py:224
  23.8 11.5 %collective-permute-start.4 = (bf16[160,896]{1,0:T(8,128)(2,1)S(1)}, bf16[160,896]{1,0:T(8,128)(2,1)S(1)}, u32[]{:S(2)}, u32[]{:S(2)}) collective-permute-start(bf16[160,896]{1,0:T(8,128)(2,1)S(1)} %bitcast.65), channel_id=1, source_target_pairs={{0,19},{4,20},{16,0},{20,5},{1,16},{5,21},{17,1},{21,6},{2,17},{6,... | collective-permute-start | bytes 860168 | tf_op jit(solution)/shard_map/ppermute | solution.py:38
  25.7 17.3 %collective-permute-start.3 = (bf16[160,896]{1,0:T(8,128)(2,1)S(1)}, bf16[160,896]{1,0:T(8,128)(2,1)S(1)}, u32[]{:S(2)}, u32[]{:S(2)}) collective-permute-start(bf16[160,896]{1,0:T(8,128)(2,1)S(1)} %bitcast.66), channel_id=1, source_target_pairs={{0,16},{4,23},{16,1},{20,4},{1,17},{5,20},{17,2},{21,5},{2,18},{6,... | collective-permute-start | bytes 860168 | tf_op jit(solution)/shard_map/ppermute | solution.py:38
  35.3 22.1 %collective-permute-start.6 = (bf16[160,896]{1,0:T(8,128)(2,1)S(1)}, bf16[160,896]{1,0:T(8,128)(2,1)S(1)}, u32[]{:S(2)}, u32[]{:S(2)}) collective-permute-start(bf16[160,896]{1,0:T(8,128)(2,1)S(1)} %collective-permute-done.4.rest_2_), channel_id=1, source_target_pairs={{0,19},{4,20},{16,0},{20,5},{1,16},{5,21},{17,1},{21,6},{2,17},{6,... | collective-permute-start | bytes 860168 | tf_op jit(solution)/shard_map/ppermute | solution.py:38
  42.9 17.7 %collective-permute-start.5 = (bf16[160,896]{1,0:T(8,128)(2,1)S(1)}, bf16[160,896]{1,0:T(8,128)(2,1)S(1)}, u32[]{:S(2)}, u32[]{:S(2)}) collective-permute-start(bf16[160,896]{1,0:T(8,128)(2,1)S(1)} %collective-permute-done.3.rest_1_), channel_id=1, source_target_pairs={{0,16},{4,23},{16,1},{20,4},{1,17},{5,20},{17,2},{21,5},{2,18},{6,... | collective-permute-start | bytes 860168 | tf_op jit(solution)/shard_map/ppermute | solution.py:38
  51.2 52.8 %collective-permute-start.14 = (bf16[80,1280]{1,0:T(8,128)(2,1)S(1)}, bf16[80,1280]{1,0:T(8,128)(2,1)S(1)}, u32[]{:S(2)}, u32[]{:S(2)}) collective-permute-start(bf16[80,1280]{1,0:T(8,128)(2,1)S(1)} %bitcast.68), channel_id=1, source_target_pairs={{0,16},{4,23},{16,1},{20,4},{1,17},{5,20},{17,2},{21,5},{2,18},{6,... | collective-permute-start | bytes 614408 | tf_op jit(solution)/shard_map/ppermute | solution.py:38
  53.1 57.1 %collective-permute-start.15 = (bf16[80,1280]{1,0:T(8,128)(2,1)S(1)}, bf16[80,1280]{1,0:T(8,128)(2,1)S(1)}, u32[]{:S(2)}, u32[]{:S(2)}) collective-permute-start(bf16[80,1280]{1,0:T(8,128)(2,1)S(1)} %bitcast.69), channel_id=1, source_target_pairs={{0,19},{4,20},{16,0},{20,5},{1,16},{5,21},{17,1},{21,6},{2,17},{6,... | collective-permute-start | bytes 614408 | tf_op jit(solution)/shard_map/ppermute | solution.py:38
  57.4 14.2 %collective-permute-start.8 = (bf16[160,896]{1,0:T(8,128)(2,1)S(1)}, bf16[160,896]{1,0:T(8,128)(2,1)S(1)}, u32[]{:S(2)}, u32[]{:S(2)}) collective-permute-start(bf16[160,896]{1,0:T(8,128)(2,1)S(1)} %collective-permute-done.6.rest_4_), channel_id=1, source_target_pairs={{0,19},{4,20},{16,0},{20,5},{1,16},{5,21},{17,1},{21,6},{2,17},{6,... | collective-permute-start | bytes 860168 | tf_op jit(solution)/shard_map/ppermute | solution.py:38
  60.6 22.1 %collective-permute-start.7 = (bf16[160,896]{1,0:T(8,128)(2,1)S(1)}, bf16[160,896]{1,0:T(8,128)(2,1)S(1)}, u32[]{:S(2)}, u32[]{:S(2)}) collective-permute-start(bf16[160,896]{1,0:T(8,128)(2,1)S(1)} %collective-permute-done.5.rest_3_), channel_id=1, source_target_pairs={{0,16},{4,23},{16,1},{20,4},{1,17},{5,20},{17,2},{21,5},{2,18},{6,... | collective-permute-start | bytes 860168 | tf_op jit(solution)/shard_map/ppermute | solution.py:38
  71.7 19.6 %collective-permute-start.10 = (bf16[80,896]{1,0:T(8,128)(2,1)S(1)}, bf16[80,896]{1,0:T(8,128)(2,1)S(1)}, u32[]{:S(2)}, u32[]{:S(2)}) collective-permute-start(bf16[80,896]{1,0:T(8,128)(2,1)S(1)} %slice.56), channel_id=1, source_target_pairs={{0,19},{4,20},{16,0},{20,5},{1,16},{5,21},{17,1},{21,6},{2,17},{6,... | collective-permute-start | bytes 430088 | tf_op jit(solution)/shard_map/ppermute | solution.py:38
  82.7 11.9 %collective-permute-start.9 = (bf16[80,896]{1,0:T(8,128)(2,1)S(1)}, bf16[80,896]{1,0:T(8,128)(2,1)S(1)}, u32[]{:S(2)}, u32[]{:S(2)}) collective-permute-start(bf16[80,896]{1,0:T(8,128)(2,1)S(1)} %slice.55), channel_id=1, source_target_pairs={{0,16},{4,23},{16,1},{20,4},{1,17},{5,20},{17,2},{21,5},{2,18},{6,... | collective-permute-start | bytes 430088 | tf_op jit(solution)/shard_map/ppermute | solution.py:38
  88.9 5.7 %copy-start.1 = (f32[1,4,2688]{2,1,0:T(4,128)S(1)}, f32[1,4,2688]{2,1,0:T(4,128)}, u32[]{:S(2)}) copy-start(f32[1,4,2688]{2,1,0:T(4,128)} %all_taps.1) | copy-start | bytes 129028
  88.9 5.7 %copy-start.2 = (f32[1,2688]{1,0:T(1,128)S(1)}, f32[1,2688]{1,0:T(1,128)}, u32[]{:S(2)}) copy-start(f32[1,2688]{1,0:T(1,128)} %all_bias.1) | copy-start | bytes 32260
  89.1 2.2 %collective-permute-start.2 = (bf16[8,1280]{1,0:T(8,128)(2,1)S(1)}, bf16[8,1280]{1,0:T(8,128)(2,1)S(1)}, u32[]{:S(2)}, u32[]{:S(2)}) collective-permute-start(bf16[8,1280]{1,0:T(8,128)(2,1)S(1)} %slice.52), channel_id=1, source_target_pairs={{0,16},{1,17},{2,18},{3,19},{4,20},{5,21},{6,22},{7,23},{8,24},{9,... | collective-permute-start | bytes 61448 | tf_op jit(solution)/shard_map/ppermute | solution.py:273
  102.5 9.6 %collective-permute-start.11 = (bf16[64,640]{1,0:T(8,128)(2,1)S(1)}, bf16[64,640]{1,0:T(8,128)(2,1)S(1)}, u32[]{:S(2)}, u32[]{:S(2)}) collective-permute-start(bf16[64,640]{1,0:T(8,128)(2,1)S(1)} %get-tuple-element.14), channel_id=1, source_target_pairs={{0,16},{1,17},{2,18},{3,19},{4,20},{5,21},{6,22},{7,23},{8,24},{9,... | collective-permute-start | bytes 245768 | tf_op jit(solution)/shard_map/ppermute | solution.py:295
  104.0 15.5 %collective-permute-start.16 = (bf16[80,1280]{1,0:T(8,128)(2,1)S(1)}, bf16[80,1280]{1,0:T(8,128)(2,1)S(1)}, u32[]{:S(2)}, u32[]{:S(2)}) collective-permute-start(bf16[80,1280]{1,0:T(8,128)(2,1)S(1)} %collective-permute-done.14.rest_1_), channel_id=1, source_target_pairs={{0,16},{4,23},{16,1},{20,4},{1,17},{5,20},{17,2},{21,5},{2,18},{6,... | collective-permute-start | bytes 614408 | tf_op jit(solution)/shard_map/ppermute | solution.py:38
  110.2 13.0 %collective-permute-start.17 = (bf16[80,1280]{1,0:T(8,128)(2,1)S(1)}, bf16[80,1280]{1,0:T(8,128)(2,1)S(1)}, u32[]{:S(2)}, u32[]{:S(2)}) collective-permute-start(bf16[80,1280]{1,0:T(8,128)(2,1)S(1)} %collective-permute-done.15.rest_2_), channel_id=1, source_target_pairs={{0,19},{4,20},{16,0},{20,5},{1,16},{5,21},{17,1},{21,6},{2,17},{6,... | collective-permute-start | bytes 614408 | tf_op jit(solution)/shard_map/ppermute | solution.py:38
  112.1 31.3 %copy-start.3 = (f32[1,2560]{1,0:T(1,128)S(1)}, f32[1,2560]{1,0:T(1,128)}, u32[]{:S(2)}) copy-start(f32[1,2560]{1,0:T(1,128)} %all_gain.1) | copy-start | bytes 30724
  112.7 13.0 %collective-permute-start.12 = (f32[4,128]{1,0:T(4,128)S(1)}, f32[4,128]{1,0:T(4,128)S(1)}, u32[]{:S(2)}, u32[]{:S(2)}) collective-permute-start(f32[4,128]{1,0:T(4,128)S(1)} %bitcast.77), channel_id=1, source_target_pairs={{0,4},{4,0},{1,5},{5,1},{2,6},{6,2},{3,7},{7,3},{8,12},{12,8},{9,1... | collective-permute-start | bytes 6152 | tf_op jit(solution)/shard_map/ppermute | solution.py:224
  119.5 9.6 %collective-permute-start.18 = (bf16[80,1280]{1,0:T(8,128)(2,1)S(1)}, bf16[80,1280]{1,0:T(8,128)(2,1)S(1)}, u32[]{:S(2)}, u32[]{:S(2)}) collective-permute-start(bf16[80,1280]{1,0:T(8,128)(2,1)S(1)} %collective-permute-done.16.rest_3_), channel_id=1, source_target_pairs={{0,16},{4,23},{16,1},{20,4},{1,17},{5,20},{17,2},{21,5},{2,18},{6,... | collective-permute-start | bytes 614408 | tf_op jit(solution)/shard_map/ppermute | solution.py:38
  123.2 10.4 %collective-permute-start.19 = (bf16[80,1280]{1,0:T(8,128)(2,1)S(1)}, bf16[80,1280]{1,0:T(8,128)(2,1)S(1)}, u32[]{:S(2)}, u32[]{:S(2)}) collective-permute-start(bf16[80,1280]{1,0:T(8,128)(2,1)S(1)} %collective-permute-done.17.rest_4_), channel_id=1, source_target_pairs={{0,19},{4,20},{16,0},{20,5},{1,16},{5,21},{17,1},{21,6},{2,17},{6,... | collective-permute-start | bytes 614408 | tf_op jit(solution)/shard_map/ppermute | solution.py:38
  125.7 13.4 %collective-permute-start.13 = (f32[4,128]{1,0:T(4,128)S(1)}, f32[4,128]{1,0:T(4,128)S(1)}, u32[]{:S(2)}, u32[]{:S(2)}) collective-permute-start(f32[4,128]{1,0:T(4,128)S(1)} %bitcast_add_fusion.1), channel_id=1, source_target_pairs={{0,8},{8,0},{1,9},{9,1},{2,10},{10,2},{3,11},{11,3},{4,12},{12,4},... | collective-permute-start | bytes 6152 | tf_op jit(solution)/shard_map/ppermute | solution.py:224
  129.1 10.1 %collective-permute-start.20 = (bf16[80,640]{1,0:T(8,128)(2,1)S(1)}, bf16[80,640]{1,0:T(8,128)(2,1)S(1)}, u32[]{:S(2)}, u32[]{:S(2)}) collective-permute-start(bf16[80,640]{1,0:T(8,128)(2,1)S(1)} %slice.57), channel_id=1, source_target_pairs={{0,16},{4,23},{16,1},{20,4},{1,17},{5,20},{17,2},{21,5},{2,18},{6,... | collective-permute-start | bytes 307208 | tf_op jit(solution)/shard_map/ppermute | solution.py:38
  133.6 9.8 %collective-permute-start.21 = (bf16[80,640]{1,0:T(8,128)(2,1)S(1)}, bf16[80,640]{1,0:T(8,128)(2,1)S(1)}, u32[]{:S(2)}, u32[]{:S(2)}) collective-permute-start(bf16[80,640]{1,0:T(8,128)(2,1)S(1)} %slice.58), channel_id=1, source_target_pairs={{0,19},{4,20},{16,0},{20,5},{1,16},{5,21},{17,1},{21,6},{2,17},{6,... | collective-permute-start | bytes 307208 | tf_op jit(solution)/shard_map/ppermute | solution.py:38
  145.5 21.0 %copy-start.7 = (bf16[1,1,128,1280]{3,2,1,0:T(8,128)(2,1)S(1)}, bf16[1,1,128,1280]{3,2,1,0:T(8,128)(2,1)}, u32[]{:S(2)}) copy-start(bf16[1,1,128,1280]{3,2,1,0:T(8,128)(2,1)} %param.11) | copy-start | bytes 983044
  145.5 9.9 %collective-permute-start.22 = (bf16[2,128,1280]{2,1,0:T(8,128)(2,1)S(1)}, bf16[2,128,1280]{2,1,0:T(8,128)(2,1)S(1)}, u32[]{:S(2)}, u32[]{:S(2)}) collective-permute-start(bf16[2,128,1280]{2,1,0:T(8,128)(2,1)S(1)} %select_bitcast_fusion), channel_id=1, source_target_pairs={{0,4},{4,0},{1,5},{5,1},{2,6},{6,2},{3,7},{7,3},{8,12},{12,8},{9,1... | collective-permute-start | bytes 1966088 | tf_op jit(solution)/shard_map/ppermute | solution.py:224
  155.7 10.8 %collective-permute-start.23 = (bf16[128,1280]{1,0:T(8,128)(2,1)S(1)}, bf16[128,1280]{1,0:T(8,128)(2,1)S(1)}, u32[]{:S(2)}, u32[]{:S(2)}) collective-permute-start(bf16[128,1280]{1,0:T(8,128)(2,1)S(1)} %fusion.36), channel_id=1, source_target_pairs={{0,8},{8,0},{1,9},{9,1},{2,10},{10,2},{3,11},{11,3},{4,12},{12,4},... | collective-permute-start | bytes 983048 | tf_op jit(solution)/shard_map/ppermute | solution.py:224
  166.6 14.1 %collective-permute-start.24 = (bf16[128,1280]{1,0:T(8,128)(2,1)S(1)}, bf16[128,1280]{1,0:T(8,128)(2,1)S(1)}, u32[]{:S(2)}, u32[]{:S(2)}) collective-permute-start(bf16[128,1280]{1,0:T(8,128)(2,1)S(1)} %fusion.34), channel_id=1, source_target_pairs={{0,32},{32,64},{64,96},{96,128},{128,160},{160,192},{192,224},{224... | collective-permute-start | bytes 983048 | tf_op jit(solution)/shard_map/ppermute | solution.py:328
  (4 other events, 22.1 us)
where the time goes:
time: 182 us; the launch traced here: 181 us
  starting transfers between devices  113 us (62%)
  waiting for transfers between devices  48.3 us (27%)
  Pallas kernels  10.2 us (6%)
  other arithmetic  4.66 us (3%)
  matrix products  2.6 us (1%)
  local copies, waits for them, and re-layouts  2.09 us (1%)
    ppermute x16, starting transfers between devices, shifted(): return lax.ppermute(x, RING, pairs)  70.2 us
    ppermute x6, starting transfers between devices, swapped(): return lax.ppermute(x, axis, [(0, 1), (1, 0)])  28.7 us
    ppermute x16, waiting for transfers between devices, shifted(): return lax.ppermute(x, RING, pairs)  25.2 us
    ppermute x1, waiting for transfers between devices, shards(): lax.ppermute(next_rows, 'section', [(i, (i + 1) % 16) for i in range(16)])  10.6 us
    ppermute x6, waiting for transfers between devices, swapped(): return lax.ppermute(x, axis, [(0, 1), (1, 0)])  10.3 us
    pallas_call x3, Pallas kernels, call(): pl.pallas_call(kernel, out_shape=outs, in_specs=[SMEM] * len(scalars) + [...  10.2 us
    all_to_all x1, starting transfers between devices, shards(): classes = lax.all_to_all(packed, ('par', 'core'), 0, 0).reshape(160, WIDE)  7.81 us
  transfers between devices with their start and end apart: 26, of which 13 were waited for; matrix products, arithmetic and copies ran while one was open for 2% of the time, Pallas kernels for 5%

commit v1 on v0

--- a/solution.py
+++ b/solution.py
@@ -23,6 +23,7 @@
 WIDE = TAPPED + 128
 ROWS = 512
 PIECE = ROWS // BLOCK
+HALF = D // 2
 
 
 def ring_index(place, core):
@@ -188,28 +189,75 @@
     state_out[...] = state.astype(jnp.bfloat16)
 
 
-def late_kernel(y_in, c_in, grown, arriving, y_out, square_out):
+def pieces(square, lane):
+    high = square.astype(jnp.bfloat16).astype(jnp.float32)
+    middle = (square - high).astype(jnp.bfloat16).astype(jnp.float32)
+    low = square - high - middle
+    split = jnp.where(lane == 0, high, jnp.where(lane == 1, middle, jnp.where(lane == 2, low, 0.0)))
+    return split.astype(jnp.bfloat16)
+
+
+def out_kernel(where, y_in, c_in, grown, arriving, all_gain, *rest):
+    chunks, (keep_x, send_x, keep_y, send_y, weight, act, square, ordered) = rest[:9], rest[9:]
+    fill(where, chunks, weight, 1)
+    gain = class_columns(all_gain[...], where[2], 320)
     y = y_in[...] + grown[...] * jnp.dot(
         c_in[...], arriving[...], preferred_element_type=jnp.float32
     )
-    y_out[...] = y
-    square_out[...] = jnp.broadcast_to(jnp.sum(y * y, axis=1, keepdims=True), (ROWS, 128))
-
-
-def out_kernel(where, y_in, square, all_gain, *rest):
-    chunks, (out, weight) = rest[:9], rest[9:]
-    fill(where, chunks, weight, 1)
-    gain = class_columns(all_gain[...], where[2], 320)
-    scale = lax.rsqrt(square[:, :1] * (1.0 / INNER) + epsilon)
-    normed = (y_in[...] * scale * gain).astype(jnp.bfloat16)
-    out[...] = jnp.dot(normed, weight[...], preferred_element_type=jnp.float32).astype(jnp.bfloat16)
+    act[...] = (y * gain).astype(jnp.bfloat16)
+    square[...] = jnp.broadcast_to(jnp.sum(y * y, axis=1, keepdims=True), (ROWS, 128))
+    par, core = where[3], where[4]
+    starts = []
+    for p in (par, 1 - par):
+        for c in (core, 1 - core):
+            starts.append(pl.multiple_of((p * 2 + c) * BLOCK, BLOCK))
+    for k in range(4):
+        ordered[k * BLOCK : (k + 1) * BLOCK, :] = act[pl.ds(starts[k], BLOCK), :]
+    lane = lax.broadcasted_iota(jnp.int32, (BLOCK, 128), 1)
+    result = jnp.dot(ordered[...], weight[...], preferred_element_type=jnp.float32)
+    for k in range(4):
+        part = result[k * BLOCK : (k + 1) * BLOCK, :]
+        total = square[pl.ds(starts[k], BLOCK), :]
+        if k % 2 == 0:
+            keep_x[k // 2, :, :HALF] = part[:, :HALF]
+            keep_x[k // 2, :, HALF:] = jnp.where(lane == 0, total, 0.0)
+            keep_y[k // 2] = part[:, HALF:]
+        else:
+            send_x[k // 2, :, :HALF] = part[:, :HALF].astype(jnp.bfloat16)
+            send_x[k // 2, :, HALF:] = pieces(total, lane)
+            send_y[k // 2] = part[:, HALF:].astype(jnp.bfloat16)
+
+
+def chip_kernel(keep, came, keep_out, send_out):
+    keep_out[...] = keep[0] + came[0].astype(jnp.float32)
+    leaving = keep[1] + came[1].astype(jnp.float32)
+    send_out[:, :HALF] = leaving[:, :HALF].astype(jnp.bfloat16)
+    if leaving.shape[1] > HALF:
+        lane = lax.broadcasted_iota(jnp.int32, (BLOCK, 128), 1)
+        total = jnp.sum(leaving[:, HALF:], axis=1, keepdims=True)
+        send_out[:, HALF:] = pieces(jnp.broadcast_to(total, (BLOCK, 128)), lane)
+
+
+def first_kernel(keep, came, rows, out, scale_out):
+    total = keep[...] + came[...].astype(jnp.float32)
+    square = jnp.sum(total[:, HALF:], axis=1, keepdims=True)
+    scale = lax.rsqrt(square * (1.0 / INNER) + epsilon)
+    scale_out[...] = jnp.broadcast_to(scale, (BLOCK, 128))
+    wide = rows[0, 0, :, :HALF].astype(jnp.float32)
+    out[...] = (wide + total[:, :HALF] * scale).astype(jnp.bfloat16)
+
+
+def second_kernel(keep, came, rows, scale, out):
+    total = keep[...] + came[...].astype(jnp.float32)
+    wide = rows[0, 0, :, HALF:].astype(jnp.float32)
+    out[...] = (wide + total * scale[:, :1]).astype(jnp.bfloat16)
 
 
 VMEM = pl.BlockSpec(memory_space=pltpu.VMEM)
 SMEM = pl.BlockSpec(memory_space=pltpu.SMEM)
 
 
-def call(kernel, outs, scratch, scalars, *arrays):
+def called(kernel, outs, scratch, scalars, *arrays):
     return pl.pallas_call(
         kernel,
         out_shape=outs,
@@ -246,7 +294,7 @@
     par, core = lax.axis_index("par"), lax.axis_index("core")
     group = par * 2 + core
     place = lax.axis_index("dp") * 2 + lax.axis_index("blk")
-    where = jnp.stack([place, 1 - 2 * core, group]).astype(jnp.int32)
+    where = jnp.stack([place, 1 - 2 * core, group, par, core]).astype(jnp.int32)
 
     out_chunks = gathered(w_out[0], 1)
     xbc, dtw = w_xbc[0], w_dt[0]
@@ -273,7 +321,7 @@
     halo = lax.ppermute(rows[ROWS - 8 :], "blk", [(0, 1)])
 
     f32, bf16 = jnp.float32, jnp.bfloat16
-    y_local, c_rows, grown, state = call(
+    y_local, c_rows, grown, state = called(
         mix_kernel,
         (
             jax.ShapeDtypeStruct((ROWS, LOCAL), f32),
@@ -293,39 +341,56 @@
         *in_chunks,
     )
     arriving = lax.ppermute(state, "blk", [(0, 1)])
-    y, square = call(
-        late_kernel,
-        (jax.ShapeDtypeStruct((ROWS, LOCAL), f32), jax.ShapeDtypeStruct((ROWS, 128), f32)),
-        [],
-        (),
+
+    shape = jax.ShapeDtypeStruct
+    wide = HALF + 128
+    keep_x, send_x, keep_y, send_y = called(
+        out_kernel,
+        (
+            shape((2, BLOCK, wide), f32),
+            shape((2, BLOCK, wide), bf16),
+            shape((2, BLOCK, HALF), f32),
+            shape((2, BLOCK, HALF), bf16),
+        ),
+        [
+            pltpu.VMEM((LOCAL, D), bf16),
+            pltpu.VMEM((ROWS, LOCAL), bf16),
+            pltpu.VMEM((ROWS, 128), f32),
+            pltpu.VMEM((ROWS, LOCAL), bf16),
+        ],
+        (where,),
         y_local,
         c_rows,
         grown,
         arriving,
-    )
-    square = square[:, 0].reshape(PIECE, BLOCK)
-    square = square + swapped(square, "core")
-    square = square + swapped(square, "par")
-    square = jnp.broadcast_to(square.reshape(ROWS, 1), (ROWS, 128))
-    partial = call(
-        out_kernel,
-        jax.ShapeDtypeStruct((ROWS, D), bf16),
-        [pltpu.VMEM((LOCAL, D), bf16)],
-        (where,),
-        y,
-        square,
         inner_gain,
         *out_chunks,
-    ).reshape(2, 2, BLOCK, D)
-
-    own = jnp.where(core == 0, partial[:, 0], partial[:, 1])
-    other = jnp.where(core == 0, partial[:, 1], partial[:, 0])
-    chip = own.astype(f32) + swapped(other, "core").astype(f32)
-    own = jnp.where(par == 0, chip[0], chip[1])
-    other = jnp.where(par == 0, chip[1], chip[0]).astype(bf16)
-    branch = own + swapped(other, "par").astype(f32)
-    next_rows = (wide + branch).astype(bf16)
-    moved = lax.ppermute(next_rows, "section", [(i, (i + 1) % 16) for i in range(16)])
+    )
+    came_x, came_y = swapped(send_x, "core"), swapped(send_y, "core")
+    keep_x, send_x = called(
+        chip_kernel, (shape((BLOCK, wide), f32), shape((BLOCK, wide), bf16)), [], (), keep_x, came_x
+    )
+    came_x = swapped(send_x, "par")
+    keep_y, send_y = called(
+        chip_kernel, (shape((BLOCK, HALF), f32), shape((BLOCK, HALF), bf16)), [], (), keep_y, came_y
+    )
+    came_y = swapped(send_y, "par")
+    next_x, scale = called(
+        first_kernel,
+        (shape((BLOCK, HALF), bf16), shape((BLOCK, 128), f32)),
+        [],
+        (),
+        keep_x,
+        came_x,
+        stream,
+    )
+    next_y = called(
+        second_kernel, shape((BLOCK, HALF), bf16), [], (), keep_y, came_y, stream, scale
+    )
+    onward = [(i, (i + 1) % 16) for i in range(16)]
+    moved_x = lax.ppermute(next_x, "section", onward)
+    moved_y = lax.ppermute(next_y, "section", onward)
+    moved = jnp.concatenate([moved_x, moved_y], axis=1)
     return moved[None, None]
 
 

time: 182 us -> 182 us (level)
  the two profiles are of different devices: /device:TPU:1 before, /device:TPU:64 now
where the time goes in v1:
time: 182 us; the launch traced here: 180 us
  starting transfers between devices  103 us (57%)
  waiting for transfers between devices  45.6 us (25%)
  Pallas kernels  11.8 us (6%)
  local copies, waits for them, and re-layouts  10.7 us (6%)
  other arithmetic  5.65 us (3%)
  matrix products  2.61 us (1%)
    ppermute x16, starting transfers between devices, shifted(): return lax.ppermute(x, RING, pairs)  74.6 us
    ppermute x16, waiting for transfers between devices, shifted(): return lax.ppermute(x, RING, pairs)  22.7 us
    ppermute x6, starting transfers between devices, swapped(): return lax.ppermute(x, axis, [(0, 1), (1, 0)])  16 us
    pallas_call x6, Pallas kernels, called(): pl.pallas_call(kernel, out_shape=outs, in_specs=[SMEM] * len(scalars) + [...  11.8 us
    ppermute x6, waiting for transfers between devices, swapped(): return lax.ppermute(x, axis, [(0, 1), (1, 0)])  8.65 us
    unnamed x38, local copies, waits for them, and re-layouts  5.97 us
    ppermute x1, waiting for transfers between devices, shards(): arriving = lax.ppermute(state, 'blk', [(0, 1)])  5.91 us
    ppermute x1, waiting for transfers between devices, shards(): moved_y = lax.ppermute(next_y, 'section', onward)  4.78 us
  transfers between devices with their start and end apart: 27, of which 11 were waited for; matrix products, arithmetic and copies ran while one was open for 4% of the time, Pallas kernels for 5%

profile of v1, /device:TPU:64, one launch (start us, length us, event | category | flops | bytes accessed | tf_op | source)
XLA Modules:
  0.0 180.4 jit_solution(16397444681930905004)
XLA Ops:
  1.9 2.6 %fusion.28 = bf16[128,1280]{1,0:T(8,128)(2,1)S(1)} fusion(s32[1280]{0:T(1024)S(1)} %get-tuple-element.39, s32[1280]{0:T(1024)S(1)} %get-tuple-element.41, s32[1280]{0:T(1024)S(1)} %get-tuple-element.37, s32[1280]{0:T(1024)S(1)} %get-tuple-element.42, s32[1280]{0:T(1024)S(1)} %get-tuple-element.38, s32[1280]{0:T(1024)S(1)} %get-tuple-element.47, ...), kind=kOutput, calls=%fused_computation.37 | convolution fusion | flops 474316800 | bytes 707072 | tf_op jit(solution)/shard_map/dot_general | solution.py:317
  4.6 3.8 %collective-permute-start = (bf16[128,1280]{1,0:T(8,128)(2,1)S(1)}, bf16[128,1280]{1,0:T(8,128)(2,1)S(1)}, u32[]{:S(2)}, u32[]{:S(2)}) collective-permute-start(bf16[128,1280]{1,0:T(8,128)(2,1)S(1)} %fusion.28), channel_id=1, source_target_pairs={{0,8},{8,0},{1,9},{9,1},{2,10},{10,2},{3,11},{11,3},{4,12},{12,4},... | collective-permute-start | bytes 983048 | tf_op jit(solution)/shard_map/ppermute | solution.py:272
  10.1 3.5 %all-to-all-start = ((bf16[4,40,896]{2,1,0:T(8,128)(2,1)}), bf16[4,40,896]{2,1,0:T(8,128)(2,1)S(1)}, u32[]{:S(2)}, u32[]{:S(2)}) async-start(bf16[4,40,896]{2,1,0:T(8,128)(2,1)} %fusion.39), calls=%async_computation | async-start | bytes 573440 | tf_op jit(solution)/shard_map/all_to_all | solution.py:306
  13.6 2.5 %collective-permute-done = bf16[128,1280]{1,0:T(8,128)(2,1)S(1)} collective-permute-done((bf16[128,1280]{1,0:T(8,128)(2,1)S(1)}, bf16[128,1280]{1,0:T(8,128)(2,1)S(1)}, u32[]{:S(2)}, u32[]{:S(2)}) %collective-permute-start) | collective-permute-done | bytes 327712 | tf_op jit(solution)/shard_map/ppermute | solution.py:272
  19.8 5.0 %collective-permute-start.4 = (bf16[160,896]{1,0:T(8,128)(2,1)S(1)}, bf16[160,896]{1,0:T(8,128)(2,1)S(1)}, u32[]{:S(2)}, u32[]{:S(2)}) collective-permute-start(bf16[160,896]{1,0:T(8,128)(2,1)S(1)} %bitcast.35), channel_id=1, source_target_pairs={{0,19},{4,20},{16,0},{20,5},{1,16},{5,21},{17,1},{21,6},{2,17},{6,... | collective-permute-start | bytes 860168 | tf_op jit(solution)/shard_map/ppermute | solution.py:39
  24.8 3.3 %collective-permute-start.3 = (bf16[160,896]{1,0:T(8,128)(2,1)S(1)}, bf16[160,896]{1,0:T(8,128)(2,1)S(1)}, u32[]{:S(2)}, u32[]{:S(2)}) collective-permute-start(bf16[160,896]{1,0:T(8,128)(2,1)S(1)} %bitcast.36), channel_id=1, source_target_pairs={{0,16},{4,23},{16,1},{20,4},{1,17},{5,20},{17,2},{21,5},{2,18},{6,... | collective-permute-start | bytes 860168 | tf_op jit(solution)/shard_map/ppermute | solution.py:39
  28.1 5.2 %collective-permute-start.12 = (bf16[80,1280]{1,0:T(8,128)(2,1)S(1)}, bf16[80,1280]{1,0:T(8,128)(2,1)S(1)}, u32[]{:S(2)}, u32[]{:S(2)}) collective-permute-start(bf16[80,1280]{1,0:T(8,128)(2,1)S(1)} %bitcast.38), channel_id=1, source_target_pairs={{0,16},{4,23},{16,1},{20,4},{1,17},{5,20},{17,2},{21,5},{2,18},{6,... | collective-permute-start | bytes 614408 | tf_op jit(solution)/shard_map/ppermute | solution.py:39
  33.3 2.9 %collective-permute-start.13 = (bf16[80,1280]{1,0:T(8,128)(2,1)S(1)}, bf16[80,1280]{1,0:T(8,128)(2,1)S(1)}, u32[]{:S(2)}, u32[]{:S(2)}) collective-permute-start(bf16[80,1280]{1,0:T(8,128)(2,1)S(1)} %bitcast.39), channel_id=1, source_target_pairs={{0,19},{4,20},{16,0},{20,5},{1,16},{5,21},{17,1},{21,6},{2,17},{6,... | collective-permute-start | bytes 614408 | tf_op jit(solution)/shard_map/ppermute | solution.py:39
  36.3 6.0 %collective-permute-start.6 = (bf16[160,896]{1,0:T(8,128)(2,1)S(1)}, bf16[160,896]{1,0:T(8,128)(2,1)S(1)}, u32[]{:S(2)}, u32[]{:S(2)}) collective-permute-start(bf16[160,896]{1,0:T(8,128)(2,1)S(1)} %collective-permute-done.4.rest_2_), channel_id=1, source_target_pairs={{0,19},{4,20},{16,0},{20,5},{1,16},{5,21},{17,1},{21,6},{2,17},{6,... | collective-permute-start | bytes 860168 | tf_op jit(solution)/shard_map/ppermute | solution.py:39
  42.3 2.1 %collective-permute-done.3.rest_1_ = bf16[160,896]{1,0:T(8,128)(2,1)S(1)} collective-permute-done((bf16[160,896]{1,0:T(8,128)(2,1)S(1)}, bf16[160,896]{1,0:T(8,128)(2,1)S(1)}, u32[]{:S(2)}, u32[]{:S(2)}) %collective-permute-start.3) | collective-permute-done | bytes 286752 | tf_op jit(solution)/shard_map/ppermute | solution.py:39
  44.4 4.9 %collective-permute-start.5 = (bf16[160,896]{1,0:T(8,128)(2,1)S(1)}, bf16[160,896]{1,0:T(8,128)(2,1)S(1)}, u32[]{:S(2)}, u32[]{:S(2)}) collective-permute-start(bf16[160,896]{1,0:T(8,128)(2,1)S(1)} %collective-permute-done.3.rest_1_), channel_id=1, source_target_pairs={{0,16},{4,23},{16,1},{20,4},{1,17},{5,20},{17,2},{21,5},{2,18},{6,... | collective-permute-start | bytes 860168 | tf_op jit(solution)/shard_map/ppermute | solution.py:39
  49.3 5.5 %collective-permute-done.12.rest_1_ = bf16[80,1280]{1,0:T(8,128)(2,1)S(1)} collective-permute-done((bf16[80,1280]{1,0:T(8,128)(2,1)S(1)}, bf16[80,1280]{1,0:T(8,128)(2,1)S(1)}, u32[]{:S(2)}, u32[]{:S(2)}) %collective-permute-start.12) | collective-permute-done | bytes 204832 | tf_op jit(solution)/shard_map/ppermute | solution.py:39
  54.8 3.3 %collective-permute-start.14 = (bf16[80,1280]{1,0:T(8,128)(2,1)S(1)}, bf16[80,1280]{1,0:T(8,128)(2,1)}, u32[]{:S(2)}, u32[]{:S(2)}) collective-permute-start(bf16[80,1280]{1,0:T(8,128)(2,1)S(1)} %collective-permute-done.12.rest_1_), channel_id=1, source_target_pairs={{0,16},{4,23},{16,1},{20,4},{1,17},{5,20},{17,2},{21,5},{2,18},{6,... | collective-permute-start | bytes 614408 | tf_op jit(solution)/shard_map/ppermute | solution.py:39
  58.8 3.4 %collective-permute-start.15 = (bf16[80,1280]{1,0:T(8,128)(2,1)S(1)}, bf16[80,1280]{1,0:T(8,128)(2,1)}, u32[]{:S(2)}, u32[]{:S(2)}) collective-permute-start(bf16[80,1280]{1,0:T(8,128)(2,1)S(1)} %collective-permute-done.13.rest_2_), channel_id=1, source_target_pairs={{0,19},{4,20},{16,0},{20,5},{1,16},{5,21},{17,1},{21,6},{2,17},{6,... | collective-permute-start | bytes 614408 | tf_op jit(solution)/shard_map/ppermute | solution.py:39
  62.9 6.3 %collective-permute-done.14.rest_3_ = bf16[80,1280]{1,0:T(8,128)(2,1)} collective-permute-done((bf16[80,1280]{1,0:T(8,128)(2,1)S(1)}, bf16[80,1280]{1,0:T(8,128)(2,1)}, u32[]{:S(2)}, u32[]{:S(2)}) %collective-permute-start.14) | collective-permute-done | bytes 204832 | tf_op jit(solution)/shard_map/ppermute | solution.py:39
  71.2 9.1 %collective-permute-start.17 = (bf16[80,1280]{1,0:T(8,128)(2,1)}, bf16[80,1280]{1,0:T(8,128)(2,1)S(1)}, u32[]{:S(2)}, u32[]{:S(2)}) collective-permute-start(bf16[80,1280]{1,0:T(8,128)(2,1)} %collective-permute-done.15.rest_4_), channel_id=1, source_target_pairs={{0,19},{4,20},{16,0},{20,5},{1,16},{5,21},{17,1},{21,6},{2,17},{6,... | collective-permute-start | bytes 614408 | tf_op jit(solution)/shard_map/ppermute | solution.py:39
  80.3 6.0 %collective-permute-start.8 = (bf16[160,896]{1,0:T(8,128)(2,1)S(1)}, bf16[160,896]{1,0:T(8,128)(2,1)S(1)}, u32[]{:S(2)}, u32[]{:S(2)}) collective-permute-start(bf16[160,896]{1,0:T(8,128)(2,1)S(1)} %collective-permute-done.6.rest_4_), channel_id=1, source_target_pairs={{0,19},{4,20},{16,0},{20,5},{1,16},{5,21},{17,1},{21,6},{2,17},{6,... | collective-permute-start | bytes 860168 | tf_op jit(solution)/shard_map/ppermute | solution.py:39
  89.5 8.8 %collective-permute-done.8.rest_6_ = bf16[160,896]{1,0:T(8,128)(2,1)S(1)} collective-permute-done((bf16[160,896]{1,0:T(8,128)(2,1)S(1)}, bf16[160,896]{1,0:T(8,128)(2,1)S(1)}, u32[]{:S(2)}, u32[]{:S(2)}) %collective-permute-start.8) | collective-permute-done | bytes 286752 | tf_op jit(solution)/shard_map/ppermute | solution.py:39
  98.9 5.4 %collective-permute-start.10 = (bf16[80,896]{1,0:T(8,128)(2,1)}, bf16[80,896]{1,0:T(8,128)(2,1)}, u32[]{:S(2)}, u32[]{:S(2)}) collective-permute-start(bf16[80,896]{1,0:T(8,128)(2,1)} %slice.32), channel_id=1, source_target_pairs={{0,19},{4,20},{16,0},{20,5},{1,16},{5,21},{17,1},{21,6},{2,17},{6,... | collective-permute-start | bytes 430088 | tf_op jit(solution)/shard_map/ppermute | solution.py:39
  105.1 2.5 %collective-permute-start.9 = (bf16[80,896]{1,0:T(8,128)(2,1)}, bf16[80,896]{1,0:T(8,128)(2,1)}, u32[]{:S(2)}, u32[]{:S(2)}) collective-permute-start(bf16[80,896]{1,0:T(8,128)(2,1)} %slice.31), channel_id=1, source_target_pairs={{0,16},{4,23},{16,1},{20,4},{1,17},{5,20},{17,2},{21,5},{2,18},{6,... | collective-permute-start | bytes 430088 | tf_op jit(solution)/shard_map/ppermute | solution.py:39
  110.4 11.7 %collective-permute-start.18 = (bf16[80,640]{1,0:T(8,128)(2,1)}, bf16[80,640]{1,0:T(8,128)(2,1)S(1)}, u32[]{:S(2)}, u32[]{:S(2)}) collective-permute-start(bf16[80,640]{1,0:T(8,128)(2,1)} %slice.33), channel_id=1, source_target_pairs={{0,16},{4,23},{16,1},{20,4},{1,17},{5,20},{17,2},{21,5},{2,18},{6,... | collective-permute-start | bytes 307208 | tf_op jit(solution)/shard_map/ppermute | solution.py:39
  129.8 8.4 %shard_map.109 = (f32[512,640]{1,0:T(8,128)S(1)}, bf16[512,64]{1,0:T(8,128)(2,1)S(1)}, f32[512,640]{1,0:T(8,128)S(1)}, bf16[64,640]{1,0:T(8,128)(2,1)S(1)}) custom-call(s32[5]{0:T(128)S(1)} %copy-done.12, bf16[512,1280]{1,0:T(8,128)(2,1)S(1)} %bitcast.34, bf16[8,1280]{1,0:T(8,128)(2,1)} %collective-permute-done.2.halo, f32[1,4,2688]{2,1,0:T(4,128)S(1)} %copy-done.9, ...), custom_call_target="tpu_custom_call" | custom-call | tf_op jit(solution)/shard_map/pallas_call | solution.py:261
  139.6 5.9 %collective-permute-done.11.arriving = bf16[64,640]{1,0:T(8,128)(2,1)S(1)} collective-permute-done((bf16[64,640]{1,0:T(8,128)(2,1)S(1)}, bf16[64,640]{1,0:T(8,128)(2,1)S(1)}, u32[]{:S(2)}, u32[]{:S(2)}) %collective-permute-start.11) | collective-permute-done | bytes 81952 | tf_op jit(solution)/shard_map/ppermute | solution.py:343
  145.6 3.0 %shard_map.110 = (f32[2,128,768]{2,1,0:T(8,128)S(1)}, bf16[2,128,768]{2,1,0:T(8,128)(2,1)S(1)}, f32[2,128,640]{2,1,0:T(8,128)S(1)}, bf16[2,128,640]{2,1,0:T(8,128)(2,1)S(1)}) custom-call(s32[5]{0:T(128)S(1)} %copy-done.12, f32[512,640]{1,0:T(8,128)S(1)} %get-tuple-element.19.y_in, bf16[512,64]{1,0:T(8,128)(2,1)S(1)} %get-tuple-element.20.c_in, ...), custom_call_target="tpu_custom_call" | custom-call | tf_op jit(solution)/shard_map/pallas_call | solution.py:261
  150.6 2.4 %collective-permute-start.23 = (bf16[2,128,640]{2,1,0:T(8,128)(2,1)S(1)}, bf16[2,128,640]{2,1,0:T(8,128)(2,1)S(1)}, u32[]{:S(2)}, u32[]{:S(2)}) collective-permute-start(bf16[2,128,640]{2,1,0:T(8,128)(2,1)S(1)} %get-tuple-element.29), channel_id=1, source_target_pairs={{0,4},{4,0},{1,5},{5,1},{2,6},{6,2},{3,7},{7,3},{8,12},{12,8},{9,1... | collective-permute-start | bytes 983048 | tf_op jit(solution)/shard_map/ppermute | solution.py:272
  155.2 3.9 %collective-permute-start.24 = (bf16[128,640]{1,0:T(8,128)(2,1)S(1)}, bf16[128,640]{1,0:T(8,128)(2,1)S(1)}, u32[]{:S(2)}, u32[]{:S(2)}) collective-permute-start(bf16[128,640]{1,0:T(8,128)(2,1)S(1)} %get-tuple-element.31), channel_id=1, source_target_pairs={{0,8},{8,0},{1,9},{9,1},{2,10},{10,2},{3,11},{11,3},{4,12},{12,4},... | collective-permute-start | bytes 491528 | tf_op jit(solution)/shard_map/ppermute | solution.py:272
  159.2 3.7 %collective-permute-done.21.came = bf16[128,768]{1,0:T(8,128)(2,1)S(1)} collective-permute-done((bf16[128,768]{1,0:T(8,128)(2,1)S(1)}, bf16[128,768]{1,0:T(8,128)(2,1)S(1)}, u32[]{:S(2)}, u32[]{:S(2)}) %collective-permute-start.21) | collective-permute-done | bytes 196640 | tf_op jit(solution)/shard_map/ppermute | solution.py:272
  163.0 2.4 %collective-permute-done.24.came = bf16[128,640]{1,0:T(8,128)(2,1)S(1)} collective-permute-done((bf16[128,640]{1,0:T(8,128)(2,1)S(1)}, bf16[128,640]{1,0:T(8,128)(2,1)S(1)}, u32[]{:S(2)}, u32[]{:S(2)}) %collective-permute-start.24) | collective-permute-done | bytes 163872 | tf_op jit(solution)/shard_map/ppermute | solution.py:272
  165.6 3.1 %collective-permute-start.25 = (bf16[128,640]{1,0:T(8,128)(2,1)S(1)}, bf16[128,640]{1,0:T(8,128)(2,1)S(1)}, u32[]{:S(2)}, u32[]{:S(2)}) collective-permute-start(bf16[128,640]{1,0:T(8,128)(2,1)S(1)} %shard_map.114), channel_id=1, source_target_pairs={{0,32},{32,64},{64,96},{96,128},{128,160},{160,192},{192,224},{224... | collective-permute-start | bytes 491528 | tf_op jit(solution)/shard_map/ppermute | solution.py:392
  168.7 3.4 %collective-permute-start.22 = (bf16[128,640]{1,0:T(8,128)(2,1)S(1)}, bf16[128,640]{1,0:T(8,128)(2,1)S(1)}, u32[]{:S(2)}, u32[]{:S(2)}) collective-permute-start(bf16[128,640]{1,0:T(8,128)(2,1)S(1)} %get-tuple-element.27), channel_id=1, source_target_pairs={{0,32},{32,64},{64,96},{96,128},{128,160},{160,192},{192,224},{224... | collective-permute-start | bytes 491528 | tf_op jit(solution)/shard_map/ppermute | solution.py:391
  172.0 4.8 %collective-permute-done.25 = bf16[128,640]{1,0:T(8,128)(2,1)S(1)} collective-permute-done((bf16[128,640]{1,0:T(8,128)(2,1)S(1)}, bf16[128,640]{1,0:T(8,128)(2,1)S(1)}, u32[]{:S(2)}, u32[]{:S(2)}) %collective-permute-start.25) | collective-permute-done | bytes 163872 | tf_op jit(solution)/shard_map/ppermute | solution.py:392
  176.8 2.8 %collective-permute-done.22 = bf16[128,640]{1,0:T(8,128)(2,1)S(1)} collective-permute-done((bf16[128,640]{1,0:T(8,128)(2,1)S(1)}, bf16[128,640]{1,0:T(8,128)(2,1)S(1)}, u32[]{:S(2)}, u32[]{:S(2)}) %collective-permute-start.22) | collective-permute-done | bytes 163872 | tf_op jit(solution)/shard_map/ppermute | solution.py:391
  (97 shorter events, 32.0 us)
Async XLA Ops:
  4.6 11.5 %collective-permute-start = (bf16[128,1280]{1,0:T(8,128)(2,1)S(1)}, bf16[128,1280]{1,0:T(8,128)(2,1)S(1)}, u32[]{:S(2)}, u32[]{:S(2)}) collective-permute-start(bf16[128,1280]{1,0:T(8,128)(2,1)S(1)} %fusion.28), channel_id=1, source_target_pairs={{0,8},{8,0},{1,9},{9,1},{2,10},{10,2},{3,11},{11,3},{4,12},{12,4},... | collective-permute-start | bytes 983048 | tf_op jit(solution)/shard_map/ppermute | solution.py:272
  10.1 9.7 %all-to-all-start = ((bf16[4,40,896]{2,1,0:T(8,128)(2,1)}), bf16[4,40,896]{2,1,0:T(8,128)(2,1)S(1)}, u32[]{:S(2)}, u32[]{:S(2)}) async-start(bf16[4,40,896]{2,1,0:T(8,128)(2,1)} %fusion.39), calls=%async_computation | async-start | bytes 573440 | tf_op jit(solution)/shard_map/all_to_all | solution.py:306
  17.1 71.2 %collective-permute-start.1 = (bf16[2,128,1280]{2,1,0:T(8,128)(2,1)}, bf16[2,128,1280]{2,1,0:T(8,128)(2,1)}, u32[]{:S(2)}, u32[]{:S(2)}) collective-permute-start(bf16[2,128,1280]{2,1,0:T(8,128)(2,1)} %pad_maximum_fusion), channel_id=1, source_target_pairs={{0,4},{4,0},{1,5},{5,1},{2,6},{6,2},{3,7},{7,3},{8,12},{12,8},{9,1... | collective-permute-start | bytes 1966088 | tf_op jit(solution)/shard_map/ppermute | solution.py:272
  19.8 16.4 %collective-permute-start.4 = (bf16[160,896]{1,0:T(8,128)(2,1)S(1)}, bf16[160,896]{1,0:T(8,128)(2,1)S(1)}, u32[]{:S(2)}, u32[]{:S(2)}) collective-permute-start(bf16[160,896]{1,0:T(8,128)(2,1)S(1)} %bitcast.35), channel_id=1, source_target_pairs={{0,19},{4,20},{16,0},{20,5},{1,16},{5,21},{17,1},{21,6},{2,17},{6,... | collective-permute-start | bytes 860168 | tf_op jit(solution)/shard_map/ppermute | solution.py:39
  24.8 19.6 %collective-permute-start.3 = (bf16[160,896]{1,0:T(8,128)(2,1)S(1)}, bf16[160,896]{1,0:T(8,128)(2,1)S(1)}, u32[]{:S(2)}, u32[]{:S(2)}) collective-permute-start(bf16[160,896]{1,0:T(8,128)(2,1)S(1)} %bitcast.36), channel_id=1, source_target_pairs={{0,16},{4,23},{16,1},{20,4},{1,17},{5,20},{17,2},{21,5},{2,18},{6,... | collective-permute-start | bytes 860168 | tf_op jit(solution)/shard_map/ppermute | solution.py:39
  28.1 26.7 %collective-permute-start.12 = (bf16[80,1280]{1,0:T(8,128)(2,1)S(1)}, bf16[80,1280]{1,0:T(8,128)(2,1)S(1)}, u32[]{:S(2)}, u32[]{:S(2)}) collective-permute-start(bf16[80,1280]{1,0:T(8,128)(2,1)S(1)} %bitcast.38), channel_id=1, source_target_pairs={{0,16},{4,23},{16,1},{20,4},{1,17},{5,20},{17,2},{21,5},{2,18},{6,... | collective-permute-start | bytes 614408 | tf_op jit(solution)/shard_map/ppermute | solution.py:39
  33.3 25.5 %collective-permute-start.13 = (bf16[80,1280]{1,0:T(8,128)(2,1)S(1)}, bf16[80,1280]{1,0:T(8,128)(2,1)S(1)}, u32[]{:S(2)}, u32[]{:S(2)}) collective-permute-start(bf16[80,1280]{1,0:T(8,128)(2,1)S(1)} %bitcast.39), channel_id=1, source_target_pairs={{0,19},{4,20},{16,0},{20,5},{1,16},{5,21},{17,1},{21,6},{2,17},{6,... | collective-permute-start | bytes 614408 | tf_op jit(solution)/shard_map/ppermute | solution.py:39
  36.3 44.0 %collective-permute-start.6 = (bf16[160,896]{1,0:T(8,128)(2,1)S(1)}, bf16[160,896]{1,0:T(8,128)(2,1)S(1)}, u32[]{:S(2)}, u32[]{:S(2)}) collective-permute-start(bf16[160,896]{1,0:T(8,128)(2,1)S(1)} %collective-permute-done.4.rest_2_), channel_id=1, source_target_pairs={{0,19},{4,20},{16,0},{20,5},{1,16},{5,21},{17,1},{21,6},{2,17},{6,... | collective-permute-start | bytes 860168 | tf_op jit(solution)/shard_map/ppermute | solution.py:39
  44.4 42.0 %collective-permute-start.5 = (bf16[160,896]{1,0:T(8,128)(2,1)S(1)}, bf16[160,896]{1,0:T(8,128)(2,1)S(1)}, u32[]{:S(2)}, u32[]{:S(2)}) collective-permute-start(bf16[160,896]{1,0:T(8,128)(2,1)S(1)} %collective-permute-done.3.rest_1_), channel_id=1, source_target_pairs={{0,16},{4,23},{16,1},{20,4},{1,17},{5,20},{17,2},{21,5},{2,18},{6,... | collective-permute-start | bytes 860168 | tf_op jit(solution)/shard_map/ppermute | solution.py:39
  54.8 14.4 %collective-permute-start.14 = (bf16[80,1280]{1,0:T(8,128)(2,1)S(1)}, bf16[80,1280]{1,0:T(8,128)(2,1)}, u32[]{:S(2)}, u32[]{:S(2)}) collective-permute-start(bf16[80,1280]{1,0:T(8,128)(2,1)S(1)} %collective-permute-done.12.rest_1_), channel_id=1, source_target_pairs={{0,16},{4,23},{16,1},{20,4},{1,17},{5,20},{17,2},{21,5},{2,18},{6,... | collective-permute-start | bytes 614408 | tf_op jit(solution)/shard_map/ppermute | solution.py:39
  58.8 12.3 %collective-permute-start.15 = (bf16[80,1280]{1,0:T(8,128)(2,1)S(1)}, bf16[80,1280]{1,0:T(8,128)(2,1)}, u32[]{:S(2)}, u32[]{:S(2)}) collective-permute-start(bf16[80,1280]{1,0:T(8,128)(2,1)S(1)} %collective-permute-done.13.rest_2_), channel_id=1, source_target_pairs={{0,19},{4,20},{16,0},{20,5},{1,16},{5,21},{17,1},{21,6},{2,17},{6,... | collective-permute-start | bytes 614408 | tf_op jit(solution)/shard_map/ppermute | solution.py:39
  69.2 40.5 %collective-permute-start.16 = (bf16[80,1280]{1,0:T(8,128)(2,1)}, bf16[80,1280]{1,0:T(8,128)(2,1)S(1)}, u32[]{:S(2)}, u32[]{:S(2)}) collective-permute-start(bf16[80,1280]{1,0:T(8,128)(2,1)} %collective-permute-done.14.rest_3_), channel_id=1, source_target_pairs={{0,16},{4,23},{16,1},{20,4},{1,17},{5,20},{17,2},{21,5},{2,18},{6,... | collective-permute-start | bytes 614408 | tf_op jit(solution)/shard_map/ppermute | solution.py:39
  71.2 50.9 %collective-permute-start.17 = (bf16[80,1280]{1,0:T(8,128)(2,1)}, bf16[80,1280]{1,0:T(8,128)(2,1)S(1)}, u32[]{:S(2)}, u32[]{:S(2)}) collective-permute-start(bf16[80,1280]{1,0:T(8,128)(2,1)} %collective-permute-done.15.rest_4_), channel_id=1, source_target_pairs={{0,19},{4,20},{16,0},{20,5},{1,16},{5,21},{17,1},{21,6},{2,17},{6,... | collective-permute-start | bytes 614408 | tf_op jit(solution)/shard_map/ppermute | solution.py:39
  80.3 18.0 %collective-permute-start.8 = (bf16[160,896]{1,0:T(8,128)(2,1)S(1)}, bf16[160,896]{1,0:T(8,128)(2,1)S(1)}, u32[]{:S(2)}, u32[]{:S(2)}) collective-permute-start(bf16[160,896]{1,0:T(8,128)(2,1)S(1)} %collective-permute-done.6.rest_4_), channel_id=1, source_target_pairs={{0,19},{4,20},{16,0},{20,5},{1,16},{5,21},{17,1},{21,6},{2,17},{6,... | collective-permute-start | bytes 860168 | tf_op jit(solution)/shard_map/ppermute | solution.py:39
  86.4 18.0 %collective-permute-start.7 = (bf16[160,896]{1,0:T(8,128)(2,1)S(1)}, bf16[160,896]{1,0:T(8,128)(2,1)S(1)}, u32[]{:S(2)}, u32[]{:S(2)}) collective-permute-start(bf16[160,896]{1,0:T(8,128)(2,1)S(1)} %collective-permute-done.5.rest_3_), channel_id=1, source_target_pairs={{0,16},{4,23},{16,1},{20,4},{1,17},{5,20},{17,2},{21,5},{2,18},{6,... | collective-permute-start | bytes 860168 | tf_op jit(solution)/shard_map/ppermute | solution.py:39
  98.9 26.4 %collective-permute-start.10 = (bf16[80,896]{1,0:T(8,128)(2,1)}, bf16[80,896]{1,0:T(8,128)(2,1)}, u32[]{:S(2)}, u32[]{:S(2)}) collective-permute-start(bf16[80,896]{1,0:T(8,128)(2,1)} %slice.32), channel_id=1, source_target_pairs={{0,19},{4,20},{16,0},{20,5},{1,16},{5,21},{17,1},{21,6},{2,17},{6,... | collective-permute-start | bytes 430088 | tf_op jit(solution)/shard_map/ppermute | solution.py:39
  105.1 20.3 %collective-permute-start.9 = (bf16[80,896]{1,0:T(8,128)(2,1)}, bf16[80,896]{1,0:T(8,128)(2,1)}, u32[]{:S(2)}, u32[]{:S(2)}) collective-permute-start(bf16[80,896]{1,0:T(8,128)(2,1)} %slice.31), channel_id=1, source_target_pairs={{0,16},{4,23},{16,1},{20,4},{1,17},{5,20},{17,2},{21,5},{2,18},{6,... | collective-permute-start | bytes 430088 | tf_op jit(solution)/shard_map/ppermute | solution.py:39
  107.7 17.7 %copy-start.10 = (f32[1,2688]{1,0:T(1,128)S(1)}, f32[1,2688]{1,0:T(1,128)}, u32[]{:S(2)}) copy-start(f32[1,2688]{1,0:T(1,128)} %all_bias.1) | copy-start | bytes 32260
  108.4 16.9 %collective-permute-start.2 = (bf16[8,1280]{1,0:T(8,128)(2,1)}, bf16[8,1280]{1,0:T(8,128)(2,1)}, u32[]{:S(2)}, u32[]{:S(2)}) collective-permute-start(bf16[8,1280]{1,0:T(8,128)(2,1)} %slice.28), channel_id=1, source_target_pairs={{0,16},{1,17},{2,18},{3,19},{4,20},{5,21},{6,22},{7,23},{8,24},{9,... | collective-permute-start | bytes 61448 | tf_op jit(solution)/shard_map/ppermute | solution.py:321
  110.4 29.2 %collective-permute-start.18 = (bf16[80,640]{1,0:T(8,128)(2,1)}, bf16[80,640]{1,0:T(8,128)(2,1)S(1)}, u32[]{:S(2)}, u32[]{:S(2)}) collective-permute-start(bf16[80,640]{1,0:T(8,128)(2,1)} %slice.33), channel_id=1, source_target_pairs={{0,16},{4,23},{16,1},{20,4},{1,17},{5,20},{17,2},{21,5},{2,18},{6,... | collective-permute-start | bytes 307208 | tf_op jit(solution)/shard_map/ppermute | solution.py:39
  122.8 16.8 %collective-permute-start.19 = (bf16[80,640]{1,0:T(8,128)(2,1)}, bf16[80,640]{1,0:T(8,128)(2,1)}, u32[]{:S(2)}, u32[]{:S(2)}) collective-permute-start(bf16[80,640]{1,0:T(8,128)(2,1)} %slice.34), channel_id=1, source_target_pairs={{0,19},{4,20},{16,0},{20,5},{1,16},{5,21},{17,1},{21,6},{2,17},{6,... | collective-permute-start | bytes 307208 | tf_op jit(solution)/shard_map/ppermute | solution.py:39
  129.7 15.8 %copy-start.4 = (bf16[1,80,1280]{2,1,0:T(8,128)(2,1)S(1)}, bf16[1,80,1280]{2,1,0:T(8,128)(2,1)}, u32[]{:S(2)}) copy-start(bf16[1,80,1280]{2,1,0:T(8,128)(2,1)} %param.21) | copy-start | bytes 614404
  129.7 15.8 %copy-start.6 = (bf16[80,1280]{1,0:T(8,128)(2,1)S(1)}, bf16[80,1280]{1,0:T(8,128)(2,1)}, u32[]{:S(2)}) copy-start(bf16[80,1280]{1,0:T(8,128)(2,1)} %copy-done.5) | copy-start | bytes 614404
  129.7 15.8 %copy-start.8 = (bf16[80,1280]{1,0:T(8,128)(2,1)S(1)}, bf16[80,1280]{1,0:T(8,128)(2,1)}, u32[]{:S(2)}) copy-start(bf16[80,1280]{1,0:T(8,128)(2,1)} %copy-done.7) | copy-start | bytes 614404
  129.7 15.8 %copy-start.11 = (f32[1,2560]{1,0:T(1,128)S(1)}, f32[1,2560]{1,0:T(1,128)}, u32[]{:S(2)}) copy-start(f32[1,2560]{1,0:T(1,128)} %all_gain.1) | copy-start | bytes 30724
  138.1 7.4 %collective-permute-start.11 = (bf16[64,640]{1,0:T(8,128)(2,1)S(1)}, bf16[64,640]{1,0:T(8,128)(2,1)S(1)}, u32[]{:S(2)}, u32[]{:S(2)}) collective-permute-start(bf16[64,640]{1,0:T(8,128)(2,1)S(1)} %get-tuple-element.22), channel_id=1, source_target_pairs={{0,16},{1,17},{2,18},{3,19},{4,20},{5,21},{6,22},{7,23},{8,24},{9,... | collective-permute-start | bytes 245768 | tf_op jit(solution)/shard_map/ppermute | solution.py:343
  148.6 4.5 %collective-permute-start.20 = (bf16[2,128,768]{2,1,0:T(8,128)(2,1)S(1)}, bf16[2,128,768]{2,1,0:T(8,128)(2,1)S(1)}, u32[]{:S(2)}, u32[]{:S(2)}) collective-permute-start(bf16[2,128,768]{2,1,0:T(8,128)(2,1)S(1)} %get-tuple-element.24), channel_id=1, source_target_pairs={{0,4},{4,0},{1,5},{5,1},{2,6},{6,2},{3,7},{7,3},{8,12},{12,8},{9,1... | collective-permute-start | bytes 1179656 | tf_op jit(solution)/shard_map/ppermute | solution.py:272
  150.6 4.5 %collective-permute-start.23 = (bf16[2,128,640]{2,1,0:T(8,128)(2,1)S(1)}, bf16[2,128,640]{2,1,0:T(8,128)(2,1)S(1)}, u32[]{:S(2)}, u32[]{:S(2)}) collective-permute-start(bf16[2,128,640]{2,1,0:T(8,128)(2,1)S(1)} %get-tuple-element.29), channel_id=1, source_target_pairs={{0,4},{4,0},{1,5},{5,1},{2,6},{6,2},{3,7},{7,3},{8,12},{12,8},{9,1... | collective-permute-start | bytes 983048 | tf_op jit(solution)/shard_map/ppermute | solution.py:272
  153.2 9.7 %collective-permute-start.21 = (bf16[128,768]{1,0:T(8,128)(2,1)S(1)}, bf16[128,768]{1,0:T(8,128)(2,1)S(1)}, u32[]{:S(2)}, u32[]{:S(2)}) collective-permute-start(bf16[128,768]{1,0:T(8,128)(2,1)S(1)} %get-tuple-element.26), channel_id=1, source_target_pairs={{0,8},{8,0},{1,9},{9,1},{2,10},{10,2},{3,11},{11,3},{4,12},{12,4},... | collective-permute-start | bytes 589832 | tf_op jit(solution)/shard_map/ppermute | solution.py:272
  155.2 10.2 %collective-permute-start.24 = (bf16[128,640]{1,0:T(8,128)(2,1)S(1)}, bf16[128,640]{1,0:T(8,128)(2,1)S(1)}, u32[]{:S(2)}, u32[]{:S(2)}) collective-permute-start(bf16[128,640]{1,0:T(8,128)(2,1)S(1)} %get-tuple-element.31), channel_id=1, source_target_pairs={{0,8},{8,0},{1,9},{9,1},{2,10},{10,2},{3,11},{11,3},{4,12},{12,4},... | collective-permute-start | bytes 491528 | tf_op jit(solution)/shard_map/ppermute | solution.py:272
  165.6 11.3 %collective-permute-start.25 = (bf16[128,640]{1,0:T(8,128)(2,1)S(1)}, bf16[128,640]{1,0:T(8,128)(2,1)S(1)}, u32[]{:S(2)}, u32[]{:S(2)}) collective-permute-start(bf16[128,640]{1,0:T(8,128)(2,1)S(1)} %shard_map.114), channel_id=1, source_target_pairs={{0,32},{32,64},{64,96},{96,128},{128,160},{160,192},{192,224},{224... | collective-permute-start | bytes 491528 | tf_op jit(solution)/shard_map/ppermute | solution.py:392
  168.7 10.9 %collective-permute-start.22 = (bf16[128,640]{1,0:T(8,128)(2,1)S(1)}, bf16[128,640]{1,0:T(8,128)(2,1)S(1)}, u32[]{:S(2)}, u32[]{:S(2)}) collective-permute-start(bf16[128,640]{1,0:T(8,128)(2,1)S(1)} %get-tuple-element.27), channel_id=1, source_target_pairs={{0,32},{32,64},{64,96},{96,128},{128,160},{160,192},{192,224},{224... | collective-permute-start | bytes 491528 | tf_op jit(solution)/shard_map/ppermute | solution.py:391
  (13 other events, 48.8 us)
